TPU v7x, 32 devices: a whole 2x2x4 slice. The times are simulated.
32 devices in a mesh: grp: 2 (over x), ha: 16 (over z, y, core).
Axes of the slice: x: 2, y: 2, z: 4, core: 2. Of those that a mesh axis runs over, the one named last changes fastest.
Arguments:
- frames: bfloat16 [4, 16, 112, 384], P('grp', 'ha'), parts along dimension 0, may hold values from -6 to 6
- cache_first: bfloat16 [4, 16, 112, 384], P('grp', 'ha'), parts along dimension 0, may hold values from -5 to 5
- cache_second: bfloat16 [4, 16, 112, 384], P('grp', 'ha'), parts along dimension 0, may hold values from -5 to 5
- gain_first: float32 [384], replicated, may hold values from 0.1 to 1.9
- gain_second: float32 [384], replicated, may hold values from 0.1 to 1.9
- bias_first: float32 [384], replicated, may hold values from -3 to 3
- bias_second: float32 [384], replicated, may hold values from -3 to 3
- weight_first: bfloat16 [10368, 384], P(None, 'ha'), may hold values from -0.0625 to 0.0625
- weight_second: bfloat16 [10368, 384], P(None, 'ha'), may hold values from -0.0625 to 0.0625
- cotangent: bfloat16 [4, 16, 112, 384], P('grp', 'ha'), parts along dimension 0, may hold values from -6 to 6
Outputs:
- output: bfloat16 [4, 16, 112, 384], P('grp', 'ha'), parts along dimension 0
- grad_frames: bfloat16 [4, 16, 112, 384], P('grp', 'ha'), parts along dimension 0
There are 2 independent parts, one for each index of `grp`. A program takes and returns all parts, laid end to end along the dimension named above; an argument that names none is the same for every part. Nothing has to cross between parts.
All inputs are finite; a program needn't handle non-finite values.
Results may differ from a plain program's by a relative error of at most 0.006.
Values may be sent and summed in bfloat16 or wider, within the bound.
No kernel may reach another device: no remote copies, remote signals or barrier semaphores. Data moves between devices by JAX's collectives and lax.ppermute only.
A program may use at most 128 MiB of HBM per device.

v0:
```python
import jax
import jax.numpy as jnp
from jax import lax
from jax.sharding import PartitionSpec as P


def extended_2(block, sides, width):
    for axis, dim in sides:
        count = lax.axis_size(axis)
        forward = [(i, i + 1) for i in range(count - 1)]
        backward = [(target, source) for source, target in forward]
        low = lax.ppermute(
            lax.slice_in_dim(block, block.shape[dim] - width, None, axis=dim), axis, forward
        )
        high = lax.ppermute(lax.slice_in_dim(block, 0, width, axis=dim), axis, backward)
        block = jnp.concatenate([low, block, high], axis=dim)
    return block


def normed_silu(values, scales):
    mean_square = jnp.mean(values * values, axis=-1, keepdims=True)
    inverse = lax.rsqrt(mean_square + 1e-06)
    normed = values * inverse * scales
    return normed * jax.nn.sigmoid(normed)


def silu_backward(values, scales, upstream):
    mean_square = jnp.mean(values * values, axis=-1, keepdims=True)
    inverse = lax.rsqrt(mean_square + 1e-06)
    normed = values * inverse * scales
    sigmoid_value = jax.nn.sigmoid(normed)
    scaled = scales * upstream * sigmoid_value * (1.0 + normed * (1.0 - sigmoid_value))
    return inverse * scaled - values * inverse**3 * jnp.mean(
        values * scaled, axis=-1, keepdims=True
    )


def tap_patches(padded, length, rows, columns, flipped):
    pieces = []
    for frame_tap in range(3):
        for row_tap in range(3):
            for col_tap in range(3):
                if flipped:
                    frame_start, row_start, col_start = (2 - frame_tap, 2 - row_tap, 2 - col_tap)
                else:
                    frame_start, row_start, col_start = (frame_tap, row_tap, col_tap)
                pieces.append(
                    padded[
                        frame_start : frame_start + length,
                        row_start : row_start + rows,
                        col_start : col_start + columns,
                    ]
                )
    return jnp.stack(pieces, axis=3)


def local(
    frames,
    cache_first,
    cache_second,
    gain_first,
    gain_second,
    bias_first,
    bias_second,
    weight_first,
    weight_second,
    cotangent,
):
    length, rows, columns, channels = frames.shape
    kernel_one, kernel_two = (
        lax.all_gather(weight_first, "ha", axis=1, tiled=True),
        lax.all_gather(weight_second, "ha", axis=1, tiled=True),
    )
    kernel_one = kernel_one.reshape(27, channels, channels)
    inputs = frames.astype(jnp.float32)
    first_act = normed_silu(inputs, gain_first).astype(jnp.bfloat16)
    extended = jnp.concatenate([cache_first, first_act], axis=0)
    padded = extended_2(extended, (("ha", 1),), 1)
    padded = jnp.pad(padded, ((0, 0), (0, 0), (1, 1), (0, 0)))
    patches = tap_patches(padded, length, rows, columns, False)
    middle = jnp.einsum("lrwtc,tco->lrwo", patches, kernel_one, preferred_element_type=jnp.float32)
    middle = (middle + bias_first).astype(jnp.bfloat16)
    middle_float = middle.astype(jnp.float32)
    kernel_two = kernel_two.reshape(27, channels, channels)
    second_act = normed_silu(middle_float, gain_second).astype(jnp.bfloat16)
    extended = jnp.concatenate([cache_second, second_act], axis=0)
    padded = extended_2(extended, (("ha", 1),), 1)
    padded = jnp.pad(padded, ((0, 0), (0, 0), (1, 1), (0, 0)))
    patches = tap_patches(padded, length, rows, columns, False)
    second_out = jnp.einsum(
        "lrwtc,tco->lrwo", patches, kernel_two, preferred_element_type=jnp.float32
    )
    output = (inputs + second_out + bias_second).astype(jnp.bfloat16)
    padded = extended_2(cotangent, (("ha", 1),), 1)
    padded = jnp.pad(padded, ((0, 2), (0, 0), (1, 1), (0, 0)))
    patches = tap_patches(padded, length, rows, columns, True)
    grad_second = jnp.einsum(
        "lrwto,tco->lrwc", patches, kernel_two, preferred_element_type=jnp.float32
    )
    grad_middle = silu_backward(middle_float, gain_second, grad_second).astype(jnp.bfloat16)
    padded = extended_2(grad_middle, (("ha", 1),), 1)
    padded = jnp.pad(padded, ((0, 2), (0, 0), (1, 1), (0, 0)))
    patches = tap_patches(padded, length, rows, columns, True)
    grad_first = jnp.einsum(
        "lrwto,tco->lrwc", patches, kernel_one, preferred_element_type=jnp.float32
    )
    grad_frames = (
        cotangent.astype(jnp.float32) + silu_backward(inputs, gain_first, grad_first)
    ).astype(jnp.bfloat16)
    return (output, grad_frames)


def solution(mesh):
    return jax.shard_map(
        local,
        mesh=mesh,
        in_specs=(
            P("grp", "ha", None, None),
            P("grp", "ha", None, None),
            P("grp", "ha", None, None),
            P(),
            P(),
            P(),
            P(),
            P(None, "ha"),
            P(None, "ha"),
            P("grp", "ha", None, None),
        ),
        out_specs=(P("grp", "ha", None, None), P("grp", "ha", None, None)),
        check_vma=False,
    )
```

profile of v0, /device:TPU:5, one launch (start us, length us, event | category | flops | bytes accessed | tf_op | source)
XLA Modules:
  0.0 222.6 jit_solution(1379792984267743407)
XLA Ops:
  8.7 1.0 fusion.91
  9.7 1.1 fusion.99
  10.8 1.0 pad_maximum_fusion
  11.8 2.6 %collective-permute-start.1 = (bf16[4,1,112,384]{3,2,0,1:T(8,128)(2,1)S(1)}, bf16[4,1,112,384]{3,2,0,1:T(8,128)(2,1)S(1)}, u32[]{:S(2)}, u32[]{:S(2)}) collective-permute-start(bf16[4,1,112,384]{3,2,0,1:T(8,128)(2,1)S(1)} %pad_maximum_fusion), channel_id=1, source_target_pairs={{1,0},{2,1},{3,2},{4,3},{5,4},{6,5},{7,6},{8,7},{9,8},{10,9},{11,1... | collective-permute-start | bytes 1032200 | tf_op jit(solution)/shard_map/ppermute | solution.py:15
  14.4 3.9 %collective-permute-start = (bf16[4,1,112,384]{3,2,0,1:T(8,128)(2,1)S(1)}, bf16[4,1,112,384]{3,2,0,1:T(8,128)(2,1)S(1)}, u32[]{:S(2)}, u32[]{:S(2)}) collective-permute-start(bf16[4,1,112,384]{3,2,0,1:T(8,128)(2,1)S(1)} %pad_maximum_fusion), channel_id=1, source_target_pairs={{0,1},{1,2},{2,3},{3,4},{4,5},{5,6},{6,7},{7,8},{8,9},{9,10},{10,1... | collective-permute-start | bytes 1032200 | tf_op jit(solution)/shard_map/ppermute | solution.py:12
  18.3 1.9 collective-permute-start.5
  20.2 4.5 %collective-permute-start.4 = (bf16[2,1,112,384]{3,2,0,1:T(8,128)(2,1)}, bf16[2,1,112,384]{3,2,0,1:T(8,128)(2,1)S(1)}, u32[]{:S(2)}, u32[]{:S(2)}) collective-permute-start(bf16[2,1,112,384]{3,2,0,1:T(8,128)(2,1)} %bitcast.545), channel_id=1, source_target_pairs={{0,1},{1,2},{2,3},{3,4},{4,5},{5,6},{6,7},{7,8},{8,9},{9,10},{10,1... | collective-permute-start | bytes 516104 | tf_op jit(solution)/shard_map/ppermute | solution.py:12
  30.5 0.8 collective-permute-done.5
  32.9 1.1 constant_dynamic-update-slice_fusion.26
  33.9 0.8 constant_dynamic-update-slice_fusion.25
  34.7 0.7 constant_dynamic-update-slice_fusion.24
  35.4 0.7 constant_dynamic-update-slice_fusion.23
  36.1 0.7 constant_dynamic-update-slice_fusion.22
  36.8 0.7 constant_dynamic-update-slice_fusion.21
  37.6 0.7 constant_dynamic-update-slice_fusion.20
  38.3 0.7 constant_dynamic-update-slice_fusion.19
  39.0 0.7 constant_dynamic-update-slice_fusion.18
  40.4 0.7 constant_dynamic-update-slice_fusion.16
  41.1 0.7 constant_dynamic-update-slice_fusion.15
  42.5 0.7 constant_dynamic-update-slice_fusion.13
  43.2 0.7 constant_dynamic-update-slice_fusion.12
  45.3 0.7 constant_dynamic-update-slice_fusion.9
  47.4 0.7 constant_dynamic-update-slice_fusion.6
  48.8 0.9 constant_dynamic-update-slice_fusion.4
  49.6 0.7 constant_dynamic-update-slice_fusion.3
  51.7 0.7 constant_dynamic-update-slice_fusion
  52.5 33.8 %all-gather.3.cloned.1.call-done = bf16[10368,384]{0,1:T(8,128)(2,1)} async-done(((bf16[10368,24]{0,1:T(8,128)(2,1)}), bf16[10368,384]{0,1:T(8,128)(2,1)}) %all-gather.3.cloned.1.call-update) | async-done | bytes 7962640 | tf_op jit(solution)/shard_map/all_gather | solution.py:71
  86.2 11.3 %copy.39 = bf16[10368,384]{1,0:T(8,128)(2,1)} copy(bf16[10368,384]{0,1:T(8,128)(2,1)} %all-gather.3.cloned.1.call-done) | data formatting | bytes 15925248 | tf_op jit(solution)/shard_map/all_gather | solution.py:71
  97.6 7.4 %multiply_reduce_fusion.1 = (f32[2,112]{1,0:T(2,128)S(1)}, f32[2,112,384]{2,1,0:T(8,128)S(1)}) fusion(f32[384]{0:T(512)S(1)} %copy-done.7, bf16[27,384,384,1]{2,1,0,3:T(8,128)(2,1)} %bitcast.528, bf16[2,1,112,27,384]{4,2,3,0,1:T(8,128)(2,1)} %constant_dynamic-update-slice_fusion), kind=kOutput, calls=%fused_computation.90 | convolution fusion | flops 1784057600 | bytes 12953984 | tf_op jit(solution)/shard_map/lrwtc,tco->lrwo/dot_general | solution.py:81
  105.0 53.7 %all-gather.5.cloned.1.call-done = bf16[10368,384]{0,1:T(8,128)(2,1)} async-done(((bf16[10368,24]{0,1:T(8,128)(2,1)}), bf16[10368,384]{0,1:T(8,128)(2,1)}) %all-gather.5.cloned.1.call-update) | async-done | bytes 7962640 | tf_op jit(solution)/shard_map/all_gather | solution.py:72
  158.7 11.3 %copy.41 = bf16[10368,384]{1,0:T(8,128)(2,1)} copy(bf16[10368,384]{0,1:T(8,128)(2,1)} %all-gather.5.cloned.1.call-done) | data formatting | bytes 15925248 | tf_op jit(solution)/shard_map/all_gather | solution.py:72
  170.0 7.7 %multiply_reduce_fusion = (f32[2,112]{1,0:T(2,128)S(1)}, f32[2,112,384]{2,1,0:T(8,128)S(1)}) fusion(f32[2,112,384]{2,1,0:T(8,128)S(1)} %get-tuple-element.11, f32[2,112]{1,0:T(2,128)S(1)} %get-tuple-element.9, bf16[27,384,384,1]{2,1,3,0:T(8,128)(2,1)} %bitcast.524, bf16[2,1,112,27,384]{4,2,0,3,1:T(8,128)(2,1)} %copy-done.5, f32[384]{0:T(512)S(1)} %copy-done.6), kind=kOutput, calls=%fused_computation.86 | convolution fusion | flops 1784745728 | bytes 13298944 | tf_op jit(solution)/shard_map/lrwto,tco->lrwc/dot_general | solution.py:97
  178.0 2.2 collective-permute-start.7
  180.2 4.3 %collective-permute-start.6 = (bf16[2,1,112,384]{3,2,0,1:T(8,128)(2,1)S(1)}, bf16[2,1,112,384]{3,2,0,1:T(8,128)(2,1)S(1)}, u32[]{:S(2)}, u32[]{:S(2)}) collective-permute-start(bf16[2,1,112,384]{3,2,0,1:T(8,128)(2,1)S(1)} %bitcast.542), channel_id=1, source_target_pairs={{0,1},{1,2},{2,3},{3,4},{4,5},{5,6},{6,7},{7,8},{8,9},{9,10},{10,1... | collective-permute-start | bytes 516104 | tf_op jit(solution)/shard_map/ppermute | solution.py:12
  185.2 1.9 collective-permute-start.3
  187.1 4.7 %collective-permute-start.2 = (bf16[4,1,112,384]{3,2,0,1:T(8,128)(2,1)S(1)}, bf16[4,1,112,384]{3,2,0,1:T(8,128)(2,1)S(1)}, u32[]{:S(2)}, u32[]{:S(2)}) collective-permute-start(bf16[4,1,112,384]{3,2,0,1:T(8,128)(2,1)S(1)} %pad_maximum_fusion.1), channel_id=1, source_target_pairs={{0,1},{1,2},{2,3},{3,4},{4,5},{5,6},{6,7},{7,8},{8,9},{9,10},{10,1... | collective-permute-start | bytes 1032200 | tf_op jit(solution)/shard_map/ppermute | solution.py:12
  192.0 0.7 constant_dynamic-update-slice_fusion.98
  192.8 0.7 constant_dynamic-update-slice_fusion.97
  194.1 0.7 constant_dynamic-update-slice_fusion.95
  194.9 0.7 constant_dynamic-update-slice_fusion.94
  196.3 0.7 constant_dynamic-update-slice_fusion.92
  197.0 0.7 constant_dynamic-update-slice_fusion.91
  198.4 0.7 constant_dynamic-update-slice_fusion.89
  200.5 0.7 constant_dynamic-update-slice_fusion.86
  202.5 0.7 constant_dynamic-update-slice_fusion.83
  204.7 5.4 %fusion.105 = (f32[2,112]{1,0:T(2,128)S(1)}, f32[2,1,112,384]{3,2,0,1:T(8,128)S(1)}) fusion(bf16[2,1,112,384]{3,2,1,0:T(8,128)(2,1)S(1)} %copy-done, f32[384]{0:T(512)S(1)} %copy-done.4, f32[2,112]{1,0:T(2,128)S(1)} %get-tuple-element.7, bf16[27,384,384,1]{2,1,3,0:T(8,128)(2,1)S(1)} %bitcast.531, ...), kind=kOutput, calls=%fused_computation.84 | convolution fusion | flops 1784831744 | bytes 13126912 | tf_op jit(solution)/shard_map/lrwto,tco->lrwc/dot_general | solution.py:104
  210.0 0.8 fusion.106
  212.5 3.3 %fusion.68 = bf16[2,1,112,384]{3,2,1,0:T(8,128)(2,1)} fusion(bf16[27,384,384,1]{2,1,3,0:T(8,128)(2,1)S(1)} %bitcast.527, bf16[2,1,112,27,384]{4,2,0,3,1:T(8,128)(2,1)S(1)} %constant_dynamic-update-slice_fusion.27, bf16[2,1,112,384]{3,2,1,0:T(8,128)(2,1)S(1)} %copy-done, f32[384]{0:T(512)S(1)} %copy-done.8), kind=kOutput, calls=%fused_computation.37 | convolution fusion | flops 1783971840 | bytes 12953088 | tf_op jit(solution)/shard_map/lrwtc,tco->lrwo/dot_general | solution.py:90
  (130 shorter events, 23.4 us)
Async XLA Ops:
  7.2 24.3 %copy-start.3 = (bf16[2,1,112,384]{3,2,1,0:T(8,128)(2,1)S(1)}, bf16[2,1,112,384]{3,2,1,0:T(8,128)(2,1)}, u32[]{:S(2)}) copy-start(bf16[2,1,112,384]{3,2,1,0:T(8,128)(2,1)} %param.19) | copy-start | bytes 516100
  7.2 79.1 %all-gather.3.cloned.1.call-start = ((), (), s32[]{:S(2)}) async-start(), calls=%async_computation | async-start | bytes 8460288 | tf_op jit(solution)/shard_map/all_gather | solution.py:71
  7.9 150.8 %all-gather.5.cloned.1.call-start = ((), (), s32[]{:S(2)}) async-start(), calls=%async_computation.1 | async-start | bytes 8460288 | tf_op jit(solution)/shard_map/all_gather | solution.py:72
  11.8 20.7 %collective-permute-start.1 = (bf16[4,1,112,384]{3,2,0,1:T(8,128)(2,1)S(1)}, bf16[4,1,112,384]{3,2,0,1:T(8,128)(2,1)S(1)}, u32[]{:S(2)}, u32[]{:S(2)}) collective-permute-start(bf16[4,1,112,384]{3,2,0,1:T(8,128)(2,1)S(1)} %pad_maximum_fusion), channel_id=1, source_target_pairs={{1,0},{2,1},{3,2},{4,3},{5,4},{6,5},{7,6},{8,7},{9,8},{10,9},{11,1... | collective-permute-start | bytes 1032200 | tf_op jit(solution)/shard_map/ppermute | solution.py:15
  14.4 18.2 %collective-permute-start = (bf16[4,1,112,384]{3,2,0,1:T(8,128)(2,1)S(1)}, bf16[4,1,112,384]{3,2,0,1:T(8,128)(2,1)S(1)}, u32[]{:S(2)}, u32[]{:S(2)}) collective-permute-start(bf16[4,1,112,384]{3,2,0,1:T(8,128)(2,1)S(1)} %pad_maximum_fusion), channel_id=1, source_target_pairs={{0,1},{1,2},{2,3},{3,4},{4,5},{5,6},{6,7},{7,8},{8,9},{9,10},{10,1... | collective-permute-start | bytes 1032200 | tf_op jit(solution)/shard_map/ppermute | solution.py:12
  18.3 13.0 %collective-permute-start.5 = (bf16[2,1,112,384]{3,2,0,1:T(8,128)(2,1)}, bf16[2,1,112,384]{3,2,0,1:T(8,128)(2,1)S(1)}, u32[]{:S(2)}, u32[]{:S(2)}) collective-permute-start(bf16[2,1,112,384]{3,2,0,1:T(8,128)(2,1)} %bitcast.544), channel_id=1, source_target_pairs={{1,0},{2,1},{3,2},{4,3},{5,4},{6,5},{7,6},{8,7},{9,8},{10,9},{11,1... | collective-permute-start | bytes 516104 | tf_op jit(solution)/shard_map/ppermute | solution.py:15
  20.2 11.2 %collective-permute-start.4 = (bf16[2,1,112,384]{3,2,0,1:T(8,128)(2,1)}, bf16[2,1,112,384]{3,2,0,1:T(8,128)(2,1)S(1)}, u32[]{:S(2)}, u32[]{:S(2)}) collective-permute-start(bf16[2,1,112,384]{3,2,0,1:T(8,128)(2,1)} %bitcast.545), channel_id=1, source_target_pairs={{0,1},{1,2},{2,3},{3,4},{4,5},{5,6},{6,7},{7,8},{8,9},{9,10},{10,1... | collective-permute-start | bytes 516104 | tf_op jit(solution)/shard_map/ppermute | solution.py:12
  25.6 6.9 %copy-start.1 = (bf16[2,1,112,384]{3,2,1,0:T(8,128)(2,1)S(1)}, bf16[2,1,112,384]{3,2,1,0:T(8,128)(2,1)}, u32[]{:S(2)}) copy-start(bf16[2,1,112,384]{3,2,1,0:T(8,128)(2,1)} %param.11) | copy-start | bytes 516100
  32.5 15.6 %copy-start.5 = (bf16[2,1,112,27,384]{4,2,0,3,1:T(8,128)(2,1)}, bf16[2,1,112,27,384]{4,2,0,3,1:T(8,128)(2,1)S(1)}, u32[]{:S(2)}) copy-start(bf16[2,1,112,27,384]{4,2,0,3,1:T(8,128)(2,1)S(1)} %constant_dynamic-update-slice_fusion.54) | copy-start | bytes 13934596
  32.5 16.3 %copy-start = (bf16[2,1,112,384]{3,2,1,0:T(8,128)(2,1)S(1)}, bf16[2,1,112,384]{3,2,1,0:T(8,128)(2,1)}, u32[]{:S(2)}) copy-start(bf16[2,1,112,384]{3,2,1,0:T(8,128)(2,1)} %param.10) | copy-start | bytes 516100
  32.5 16.3 %copy-start.4 = (f32[384]{0:T(512)S(1)}, f32[384]{0:T(512)}, u32[]{:S(2)}) copy-start(f32[384]{0:T(512)} %param.13) | copy-start | bytes 4612
  52.5 45.1 %copy-start.7 = (f32[384]{0:T(512)S(1)}, f32[384]{0:T(512)}, u32[]{:S(2)}) copy-start(f32[384]{0:T(512)} %param.15) | copy-start | bytes 4612
  105.0 65.0 %copy-start.6 = (f32[384]{0:T(512)S(1)}, f32[384]{0:T(512)}, u32[]{:S(2)}) copy-start(f32[384]{0:T(512)} %param.14) | copy-start | bytes 4612
  170.0 34.7 %slice-start.2 = ((s8[7962624]{0:T(1024)(128)(4,1)}), s8[4194304]{0:T(1024)(128)(4,1)S(1)}, s32[]{:S(2)}) async-start(s8[7962624]{0:T(1024)(128)(4,1)} %bitcast.529), calls=%async_computation.4 | async-start | bytes 8388608
  170.0 15.2 %copy-start.2 = (bf16[2,1,112,384]{3,2,1,0:T(8,128)(2,1)S(1)}, bf16[2,1,112,384]{3,2,1,0:T(8,128)(2,1)}, u32[]{:S(2)}) copy-start(bf16[2,1,112,384]{3,2,1,0:T(8,128)(2,1)} %param.12) | copy-start | bytes 516100
  170.0 34.6 %slice-start.3 = ((s8[7962624]{0:T(1024)(128)(4,1)}), s8[3768320]{0:T(1024)(128)(4,1)S(1)}, s32[]{:S(2)}) async-start(s8[7962624]{0:T(1024)(128)(4,1)} %bitcast.529), calls=%async_computation.5 | async-start | bytes 7536640
  178.0 13.9 %collective-permute-start.7 = (bf16[2,1,112,384]{3,2,0,1:T(8,128)(2,1)S(1)}, bf16[2,1,112,384]{3,2,0,1:T(8,128)(2,1)S(1)}, u32[]{:S(2)}, u32[]{:S(2)}) collective-permute-start(bf16[2,1,112,384]{3,2,0,1:T(8,128)(2,1)S(1)} %bitcast.541), channel_id=1, source_target_pairs={{1,0},{2,1},{3,2},{4,3},{5,4},{6,5},{7,6},{8,7},{9,8},{10,9},{11,1... | collective-permute-start | bytes 516104 | tf_op jit(solution)/shard_map/ppermute | solution.py:15
  180.2 11.7 %collective-permute-start.6 = (bf16[2,1,112,384]{3,2,0,1:T(8,128)(2,1)S(1)}, bf16[2,1,112,384]{3,2,0,1:T(8,128)(2,1)S(1)}, u32[]{:S(2)}, u32[]{:S(2)}) collective-permute-start(bf16[2,1,112,384]{3,2,0,1:T(8,128)(2,1)S(1)} %bitcast.542), channel_id=1, source_target_pairs={{0,1},{1,2},{2,3},{3,4},{4,5},{5,6},{6,7},{7,8},{8,9},{9,10},{10,1... | collective-permute-start | bytes 516104 | tf_op jit(solution)/shard_map/ppermute | solution.py:12
  185.2 25.7 %collective-permute-start.3 = (bf16[4,1,112,384]{3,2,0,1:T(8,128)(2,1)S(1)}, bf16[4,1,112,384]{3,2,0,1:T(8,128)(2,1)S(1)}, u32[]{:S(2)}, u32[]{:S(2)}) collective-permute-start(bf16[4,1,112,384]{3,2,0,1:T(8,128)(2,1)S(1)} %pad_maximum_fusion.1), channel_id=1, source_target_pairs={{1,0},{2,1},{3,2},{4,3},{5,4},{6,5},{7,6},{8,7},{9,8},{10,9},{11,1... | collective-permute-start | bytes 1032200 | tf_op jit(solution)/shard_map/ppermute | solution.py:15
  187.1 23.8 %collective-permute-start.2 = (bf16[4,1,112,384]{3,2,0,1:T(8,128)(2,1)S(1)}, bf16[4,1,112,384]{3,2,0,1:T(8,128)(2,1)S(1)}, u32[]{:S(2)}, u32[]{:S(2)}) collective-permute-start(bf16[4,1,112,384]{3,2,0,1:T(8,128)(2,1)S(1)} %pad_maximum_fusion.1), channel_id=1, source_target_pairs={{0,1},{1,2},{2,3},{3,4},{4,5},{5,6},{6,7},{7,8},{8,9},{9,10},{10,1... | collective-permute-start | bytes 1032200 | tf_op jit(solution)/shard_map/ppermute | solution.py:12
  204.6 7.8 %slice-start = ((s8[7962624]{0:T(1024)(128)(4,1)}), s8[4194304]{0:T(1024)(128)(4,1)S(1)}, s32[]{:S(2)}) async-start(s8[7962624]{0:T(1024)(128)(4,1)} %bitcast.525), calls=%async_computation.2 | async-start | bytes 8388608
  204.6 7.8 %slice-start.1 = ((s8[7962624]{0:T(1024)(128)(4,1)}), s8[3768320]{0:T(1024)(128)(4,1)S(1)}, s32[]{:S(2)}) async-start(s8[7962624]{0:T(1024)(128)(4,1)} %bitcast.525), calls=%async_computation.3 | async-start | bytes 7536640
  211.2 1.2 copy-start.8
Sparse Core Ops, SparseCore 0:
  10.2 76.0 all-gather.2
  88.4 70.2 all-gather.4
where the time goes:
time: 223 us
  waiting for transfers between devices  89.8 us (40%)
  local copies, waits for them, and re-layouts  61.4 us (28%)
  starting transfers between devices  26.1 us (12%)
  matrix products  23.8 us (11%)
  between operations  14.6 us (7%)
  other arithmetic  6.78 us (3%)
    all_gather x1, waiting for transfers between devices, local(): lax.all_gather(weight_second, 'ha', axis=1, tiled=True)  53.7 us
    unnamed x127, local copies, waits for them, and re-layouts  37.3 us
    all_gather x1, waiting for transfers between devices, local(): lax.all_gather(weight_first, 'ha', axis=1, tiled=True)  33.8 us
    ppermute x4, starting transfers between devices, extended_2(): lax.ppermute(lax.slice_in_dim(block, block.shape[dim] - width, None, axis...  17.4 us
    all_gather x1, local copies, waits for them, and re-layouts, local(): lax.all_gather(weight_first, 'ha', axis=1, tiled=True)  11.3 us
    all_gather x1, local copies, waits for them, and re-layouts, local(): lax.all_gather(weight_second, 'ha', axis=1, tiled=True)  11.3 us
    ppermute x4, starting transfers between devices, extended_2(): lax.ppermute(lax.slice_in_dim(block, 0, width, axis=dim), axis, backward)  8.6 us
    dot_general x1, matrix products, local(): jnp.einsum('lrwto,tco->lrwc', patches, kernel_two, preferred_element_type...  7.75 us
  transfers between devices with their start and end apart: 10, of which 4 were waited for; matrix products, arithmetic and copies ran while one was open for 31% of the time, Pallas kernels for 0%

commit v1 on v0

v1 whole, which is shorter than its diff:
```python
import functools

import jax
import jax.numpy as jnp
from jax import lax
from jax.experimental import pallas as pl
from jax.experimental.pallas import tpu as pltpu
from jax.sharding import PartitionSpec as P


TILES = 81
SOLE = 32
HALF = SOLE // 2
MID = (TILES - 2 * SOLE + 1) // 2
VMEM_LIMIT = 12 * 1024 * 1024


def normed_silu(values, scales):
    mean_square = jnp.mean(values * values, axis=-1, keepdims=True)
    normed = values * lax.rsqrt(mean_square + 1e-06) * scales
    return normed * jax.nn.sigmoid(normed)


def silu_backward(values, scales, upstream):
    mean_square = jnp.mean(values * values, axis=-1, keepdims=True)
    inverse = lax.rsqrt(mean_square + 1e-06)
    normed = values * inverse * scales
    sigmoid_value = jax.nn.sigmoid(normed)
    scaled = scales * upstream * sigmoid_value * (1.0 + normed * (1.0 - sigmoid_value))
    return inverse * scaled - values * inverse**3 * jnp.mean(
        values * scaled, axis=-1, keepdims=True
    )


def shifted(block, by):
    zero = jnp.zeros_like(block[:, :1])
    if by > 0:
        return jnp.concatenate([zero, block[:, :-1]], axis=1)
    return jnp.concatenate([block[:, 1:], zero], axis=1)


def joined(parts_ref, length, columns, signs):
    parts = [parts_ref[k].reshape(length, columns, -1) for k in range(3)]
    return shifted(parts[0], signs) + parts[1] + shifted(parts[2], -signs)


def forward_dot(left, weight_ref, frame_tap, row_tap, col_tap):
    frames, columns, channels = left.shape
    start = (9 * frame_tap + 3 * row_tap + col_tap) * channels
    if not isinstance(start, int):
        start = pl.multiple_of(start, 128)
    return lax.dot_general(
        left.reshape(frames * columns, channels),
        weight_ref[:, pl.ds(start, channels)],
        (((1,), (1,)), ((), ())),
        preferred_element_type=jnp.float32,
    )


def backward_dot(left, weight_ref, frame_tap, row_tap, col_tap):
    frames, columns, channels = left.shape
    start = (9 * frame_tap + 3 * row_tap + col_tap) * channels
    if not isinstance(start, int):
        start = pl.multiple_of(start, 128)
    return lax.dot_general(
        left.reshape(frames * columns, channels),
        weight_ref[:, pl.ds(start, channels)],
        (((1,), (0,)), ((), ())),
        preferred_element_type=jnp.float32,
    )


def conv_forward(rows_ref, weight_ref, total_ref):
    length = rows_ref.shape[1] - 2
    for col_tap in range(3):
        for frame_tap in range(3):
            for row_tap in range(3):
                left = rows_ref[row_tap, frame_tap : frame_tap + length]
                product = forward_dot(left, weight_ref, frame_tap, row_tap, col_tap)
                if frame_tap == 0 and row_tap == 0:
                    total_ref[col_tap] = product
                else:
                    total_ref[col_tap] += product


def conv_backward(rows, weight_ref, total_ref, fresh):
    length, columns, _ = rows[0][1].shape
    for col_tap in range(3):
        start = fresh
        for row_tap, source in rows:
            for shift in range(min(3, length)):
                count = (length - shift) * columns
                product = backward_dot(source[shift:], weight_ref, 2 - shift, row_tap, col_tap)
                if start:
                    total_ref[col_tap] = product
                    start = False
                else:
                    total_ref[col_tap, :count] += product


def prepare_kernel(cache, frames, near, far, gain, rows):
    length = frames.shape[0]
    scales = gain[...][None, None]
    near_row, far_row = sides()
    for row, source in ((near_row, near), (1, None), (far_row, far)):
        rows[row, :2] = cache[...] if source is None else source[:2]
        values = frames[...] if source is None else source[2 : 2 + length]
        rows[row, 2:] = normed_silu(values.astype(jnp.float32), scales).astype(jnp.bfloat16)


def start_copies(pieces, sources, ring, weights, sems):
    width = weights[0].shape[1] // TILES
    copies = ([], [])
    for conv in range(2):
        for found in placements(pieces, sources, ring, width, conv):
            source, row, column, height, span = found
            target = weights[conv].at[pl.ds(row, height), pl.ds(column, span)]
            one = pltpu.make_async_copy(source, target, sems.at[conv, len(copies[conv])])
            one.start()
            copies[conv].append(one)
    return copies


def place_kernel(pieces, ring, *refs):
    sources, refs = refs[: len(pieces)], refs[-3:]
    copies = start_copies(pieces, sources, ring, refs[:2], refs[2])
    for one in copies[0] + copies[1]:
        one.wait()


def first_kernel(pieces, ring, rows, bias, gain, *refs):
    sources, refs = refs[: len(pieces)], refs[-6:]
    middle, act, weight_first, weight_second, total, sems = refs
    length, columns, _ = act.shape
    copies = start_copies(pieces, sources, ring, (weight_first, weight_second), sems)
    for one in copies[0]:
        one.wait()
    conv_forward(rows, weight_first, total)
    result = (joined(total, length, columns, 1) + bias[...][None, None]).astype(jnp.bfloat16)
    middle[...] = result
    act[...] = normed_silu(result.astype(jnp.float32), gain[...][None, None]).astype(jnp.bfloat16)
    for one in copies[1]:
        one.wait()


def second_kernel(cotangent, near, far, middle, gain, weight, grad, total):
    length, columns, _ = cotangent.shape
    span = slice(2 + length, 2 + 2 * length)
    near_row, far_row = sides()
    halo = ((1, cotangent[...]), (2 - near_row, near[span]), (2 - far_row, far[span]))
    conv_backward(halo, weight, total, True)
    upstream = joined(total, length, columns, -1)
    values = middle[...].astype(jnp.float32)
    grad[...] = silu_backward(values, gain[...][None, None], upstream).astype(jnp.bfloat16)


def third_kernel(
    cache, act, near, far, act_near, act_far, frames, bias, grad, weight_first, weight_second, *refs
):
    out, back_total, rows, total = refs
    length, columns, _ = act.shape
    past = slice(2 + 2 * length, 4 + 2 * length)
    near_row, far_row = sides()
    for row, older, newer in (
        (1, cache[...], act),
        (near_row, near[past], act_near),
        (far_row, far[past], act_far),
    ):
        rows[row, :2] = older
        rows[row, 2:] = newer[...]
    conv_backward(((1, grad[...]),), weight_first, back_total, True)
    conv_forward(rows, weight_second, total)
    result = joined(total, length, columns, 1) + bias[...][None, None]
    out[...] = (frames[...].astype(jnp.float32) + result).astype(jnp.bfloat16)


def fourth_kernel(near, far, frames, cotangent, gain, weight, total_in, grad_frames, total):
    length, columns, _ = frames.shape
    near_row, far_row = sides()
    total[...] = total_in[...]
    conv_backward(((2 - near_row, near[...]), (2 - far_row, far[...])), weight, total, False)
    upstream = joined(total, length, columns, -1)
    back = silu_backward(frames[...].astype(jnp.float32), gain[...][None, None], upstream)
    grad_frames[...] = (cotangent[...].astype(jnp.float32) + back).astype(jnp.bfloat16)


def call(body, outs, operands, flops, scratch=(), spaces=(), aliases=()):
    spec = pl.BlockSpec(memory_space=pltpu.VMEM)
    specs = [spec] * (len(operands) - len(spaces)) + list(spaces)
    return pl.pallas_call(
        body,
        out_shape=outs,
        in_specs=specs,
        out_specs=[spec] * len(outs),
        scratch_shapes=scratch,
        input_output_aliases=dict(aliases),
        compiler_params=pltpu.CompilerParams(vmem_limit_bytes=VMEM_LIMIT),
        cost_estimate=pl.CostEstimate(flops=flops, bytes_accessed=2**22, transcendentals=0),
    )(*operands)


def placements(pieces, sources, ring, width, conv):
    if ring == 0:
        return [(source, 0, 0, *source.shape) for source in sources[conv : conv + 1]]
    index = lax.axis_index("ha")
    core, side, turn = lax.rem(index, 2), lax.rem(index // 2, 2), index // 4
    pair = lax.rem(lax.axis_index("grp"), 2)
    found = []
    for (blocks, kind, crossed), source in zip(pieces, sources):
        whose = 1 - core if crossed else core
        for at, block in enumerate(blocks):
            block_conv, back, flip, height = block
            if block_conv != conv:
                continue
            chip = 2 * lax.rem(turn - back + ring, ring) + (1 - side if flip else side)
            begin = sum(b[3] for b in blocks[:at])
            part = pl.ds(begin, height)
            if kind == "own":
                column, span, skip = 0, TILES, 0
            elif kind == "middle" and not crossed:
                column, span, skip = SOLE + (MID - 1) * whose, MID, 0
            elif kind == "middle":
                column, span, skip = SOLE + MID * whose, MID - 1, whose
            else:
                where = 1 - pair if kind == "passed" else pair
                column, span, skip = (TILES - SOLE) * where + HALF * whose, HALF, 0
            if not isinstance(skip, int):
                skip = pl.multiple_of(skip * width, 128)
            if not isinstance(column, int):
                column = pl.multiple_of(column * width, 128)
            row = pl.multiple_of(chip * height, height)
            found.append(
                (source.at[part, pl.ds(skip, span * width)], row, column, height, span * width)
            )
    return found


def gather(shards):
    count, groups = lax.axis_size("ha"), lax.axis_size("grp")
    rows, wide = shards[0].shape
    if count % 4 or groups % 2 or (2 * rows) % 16:
        whole = [lax.all_gather(shard, "ha", axis=0, tiled=True) for shard in shards]
        return whole, [None, None], 0, [0, 0]
    ring = count // 4
    width = wide // TILES
    chip = 2 * rows

    turn = lambda a: lax.ppermute(a, "ha", [(i, (i + 4) % count) for i in range(count)])
    side = lambda a: lax.ppermute(a, "ha", [(i, i ^ 2) for i in range(count)])
    cross = lambda a: lax.ppermute(a, "ha", [(i, i ^ 1) for i in range(count)])
    over = lambda a: lax.ppermute(a, "grp", [(i, i ^ 1) for i in range(groups)])
    core = lax.axis_index("ha") % 2
    pair = lax.axis_index("grp") % 2
    others = [cross(shard) for shard in shards]

    own = [
        jnp.concatenate([jnp.where(core == 0, a, b), jnp.where(core == 0, b, a)], axis=0)
        for a, b in zip(shards, others)
    ]

    def chosen(start, taps):
        return jnp.concatenate(
            [lax.dynamic_slice_in_dim(o, start * width, taps * width, axis=1) for o in own], axis=0
        )

    ends = chosen((TILES - SOLE) * pair + HALF * core, HALF)
    mids = chosen(SOLE + (MID - 1) * core, MID)
    arrays, pieces, stages = [], [], []

    def keep(array, blocks, kind, stage):
        arrays.append(array)
        pieces.append((blocks, kind, False))
        arrays.append(cross(array))
        pieces.append((blocks, kind, True))
        stages.extend([stage, stage])

    ends_across = side(ends)
    ends_next = turn(ends)
    mids_across = side(mids)
    for conv in range(2):
        arrays.append(own[conv])
        pieces.append(([(conv, 0, False, chip)], "own", False))
        stages.append(0)
    keep(mids_across, [(0, 0, True, chip), (1, 0, True, chip)], "middle", 0)
    mids = jnp.concatenate([mids, mids_across], axis=0)
    for step in range(1, ring + 1):
        blocks = [(0, step - 1, True, chip), (1, step - 1, True, chip)]
        both = ends_across
        if step < ring:
            ends = ends_next
            blocks = [(0, step, False, chip), (1, step, False, chip)] + blocks
            both = jnp.concatenate([ends, ends_across], axis=0)
        keep(both, blocks, "ends", step)
        keep(over(both), blocks, "passed", step + 1)
        if step < ring:
            ends_across = side(ends)
            if step + 1 < ring:
                ends_next = turn(ends)
            mids = turn(mids)
            chips = [(conv, step, flip, chip) for flip in (False, True) for conv in range(2)]
            keep(mids, chips, "middle", step + 1)
    groups = [(stage > ring // 2) + (stage > ring) for stage in stages]
    return arrays, pieces, ring, groups


def neighbours(block):
    count = lax.axis_size("ha")
    inner = [(i, i ^ 1) for i in range(count)]
    outer = [(i, i + 1) for i in range(1, count - 1, 2)]
    outer += [(target, source) for source, target in outer]
    near = lax.ppermute(block, "ha", inner)
    far = lax.ppermute(block, "ha", outer)
    return near, far


def sides():
    core = lax.rem(lax.axis_index("ha"), 2)
    return 2 * (1 - core), 2 * core


def local(
    frames,
    cache_first,
    cache_second,
    gain_first,
    gain_second,
    bias_first,
    bias_second,
    weight_first,
    weight_second,
    cotangent,
):
    shape = frames.shape
    length, _, columns, channels = shape
    flat = (length, columns, channels)
    frames, cotangent = frames.reshape(flat), cotangent.reshape(flat)
    cache_first = cache_first.reshape(2, columns, channels)
    cache_second = cache_second.reshape(2, columns, channels)
    near, far = neighbours(jnp.concatenate([cache_first, frames, cotangent, cache_second], axis=0))
    arrays, pieces, ring, groups = gather([weight_first.T, weight_second.T])
    shape_of = lambda *dims: jax.ShapeDtypeStruct(dims, jnp.bfloat16)
    unit = 2 * columns * channels * channels
    totals = (3, length * columns, channels)
    total_of = jax.ShapeDtypeStruct(totals, jnp.float32)
    (rows,) = call(
        prepare_kernel,
        [shape_of(3, length + 2, columns, channels)],
        (cache_first, frames, near, far, gain_first),
        unit,
    )
    whole = [pltpu.VMEM((channels, 27 * channels), jnp.bfloat16)] * 2
    in_hbm = pl.BlockSpec(memory_space=pltpu.HBM)
    in_vmem = pl.BlockSpec(memory_space=pltpu.VMEM)
    kernels = []
    for group in range(2):
        these = [at for at in range(len(arrays)) if groups[at] == group]
        if not these:
            continue
        kernels = call(
            functools.partial(place_kernel, [pieces[at] for at in these], ring),
            whole,
            [arrays[at] for at in these] + kernels,
            unit * 9,
            [pltpu.SemaphoreType.DMA((2, 4 * len(these)))],
            [in_hbm] * len(these) + [in_vmem] * len(kernels),
            [(len(these) + at, at) for at in range(len(kernels))],
        )
        kernels = [pltpu.with_memory_space_constraint(k, pltpu.VMEM) for k in kernels]
    rest = [at for at in range(len(arrays)) if groups[at] == 2]
    scratch = pltpu.VMEM(totals, jnp.float32)
    middle, act, kernel_one, kernel_two = call(
        functools.partial(first_kernel, [pieces[at] for at in rest], ring),
        [shape_of(*flat)] * 2 + whole,
        (rows, bias_first, gain_second, *[arrays[at] for at in rest], *kernels),
        unit * 27 * length,
        [scratch, pltpu.SemaphoreType.DMA((2, 4 * len(arrays)))],
        [in_hbm] * len(rest) + [in_vmem] * 2,
        ((3 + len(rest), 2), (4 + len(rest), 3)),
    )
    kernel_one, kernel_two = (
        pltpu.with_memory_space_constraint(k, pltpu.VMEM) for k in (kernel_one, kernel_two)
    )
    act_near, act_far = neighbours(act)
    (grad,) = call(
        second_kernel,
        [shape_of(*flat)],
        (cotangent, near, far, middle, gain_second, kernel_two),
        unit * 9 * (2 * length - 1),
        [scratch],
    )
    grad_near, grad_far = neighbours(grad)
    out, back_total = call(
        third_kernel,
        [shape_of(*flat), total_of],
        (
            cache_second,
            act,
            near,
            far,
            act_near,
            act_far,
            frames,
            bias_second,
            grad,
            kernel_one,
            kernel_two,
        ),
        unit * 30 * length,
        [pltpu.VMEM((3, length + 2, columns, channels), jnp.bfloat16), scratch],
    )
    (grad_frames,) = call(
        fourth_kernel,
        [shape_of(*flat)],
        (grad_near, grad_far, frames, cotangent, gain_first, kernel_one, back_total),
        unit * 6 * (2 * length - 1),
        [scratch],
    )
    return out.reshape(shape), grad_frames.reshape(shape)


def solution(mesh):
    rows = P("grp", "ha", None, None)

    return jax.shard_map(
        local,
        mesh=mesh,
        in_specs=(rows, rows, rows, P(), P(), P(), P(), P(None, "ha"), P(None, "ha"), rows),
        out_specs=(rows, rows),
        check_vma=False,
    )
```

time: 223 us -> 143 us (0.64)
  local copies, waits for them, and re-layouts: 61.4 us -> 0.21 us
  matrix products: 23.8 us -> 0 us
  Pallas kernels: 0 us -> 20.4 us
  waiting for transfers between devices: 89.8 us -> 72.8 us
  starting transfers between devices: 26.1 us -> 42.1 us
  between operations: 14.6 us -> 1.03 us
  other arithmetic: 6.78 us -> 3.83 us
    all_gather x2 -> x0, waiting for transfers between devices: 87.5 us -> none  [the longest x1 53.7 us: local(): lax.all_gather(weight_second, 'ha', axis=1, tiled=True)]
    ppermute x8 -> x35, waiting for transfers between devices: 0.99 us -> 72.8 us  [the longest x6 41.9 us: gather(): lax.ppermute(a, 'ha', [(i, (i + 4) % count) for i in range(count)])]
    unnamed x127 -> x19, local copies, waits for them, and re-layouts: 37.3 us -> 0.13 us
    dot_general x4 -> x0, matrix products: 23.8 us -> none  [the longest x1 7.75 us: local(): jnp.einsum('lrwto,tco->lrwc', patches, kernel_two, preferred_element_type...]
    all_gather x2 -> x0, local copies, waits for them, and re-layouts: 22.6 us -> none  [the longest x1 11.3 us: local(): lax.all_gather(weight_first, 'ha', axis=1, tiled=True)]
    pallas_call x0 -> x7, Pallas kernels: none -> 20.4 us  [call(): pl.pallas_call(body, out_shape=outs, in_specs=specs, out_specs=[spec] * l...]
    ppermute x8 -> x35, starting transfers between devices: 26 us -> 42.1 us  [the longest x3 13.5 us: neighbours(): far = lax.ppermute(block, 'ha', outer)]
    unnamed x6 -> x0, other arithmetic: 2.45 us -> none
  transfers between devices with their start and end apart: 10 -> 35, of which waited for: 4 -> 12; matrix products, arithmetic and copies ran while one was open for 31% -> 3% of each run, Pallas kernels for 0% -> 9%
where the time goes in v1:
time: 143 us; the launch traced here: 140 us
  waiting for transfers between devices  72.8 us (51%)
  starting transfers between devices  42.1 us (29%)
  Pallas kernels  20.4 us (14%)
  other arithmetic  3.83 us (3%)
    ppermute x6, waiting for transfers between devices, gather(): lax.ppermute(a, 'ha', [(i, (i + 4) % count) for i in range(count)])  41.9 us
    pallas_call x7, Pallas kernels, call(): pl.pallas_call(body, out_shape=outs, in_specs=specs, out_specs=[spec] * l...  20.4 us
    ppermute x5, waiting for transfers between devices, gather(): side = lambda a: lax.ppermute(a, 'ha', [(i, i ^ 2) for i in range(count)])  16.9 us
    ppermute x3, starting transfers between devices, neighbours(): far = lax.ppermute(block, 'ha', outer)  13.5 us
    ppermute x4, waiting for transfers between devices, gather(): over = lambda a: lax.ppermute(a, 'grp', [(i, i ^ 1) for i in range(groups)])  13 us
    ppermute x14, starting transfers between devices, gather(): cross = lambda a: lax.ppermute(a, 'ha', [(i, i ^ 1) for i in range(count)])  8.48 us
    ppermute x6, starting transfers between devices, gather(): lax.ppermute(a, 'ha', [(i, (i + 4) % count) for i in range(count)])  7.75 us
    ppermute x5, starting transfers between devices, gather(): side = lambda a: lax.ppermute(a, 'ha', [(i, i ^ 2) for i in range(count)])  6.01 us
  transfers between devices with their start and end apart: 35, of which 12 were waited for; matrix products, arithmetic and copies ran while one was open for 3% of the time, Pallas kernels for 9%

profile of v1, /device:TPU:5, one launch (start us, length us, event | category | flops | bytes accessed | tf_op | source)
XLA Modules:
  0.0 140.4 jit_solution(5391088031649729477)
XLA Ops:
  0.6 0.7 collective-permute-start.2
  1.4 0.1 collective-permute-start.3
  1.5 1.3 pad_maximum_fusion.2
  2.7 0.5 collective-permute-start
  3.2 1.1 broadcast_select_fusion.2
  4.3 1.1 broadcast_select_fusion
  5.7 1.6 %collective-permute-start.4 = (bf16[96,2048]{1,0:T(8,128)(2,1)S(1)}, bf16[96,2048]{1,0:T(8,128)(2,1)S(1)}, u32[]{:S(2)}, u32[]{:S(2)}) collective-permute-start(bf16[96,2048]{1,0:T(8,128)(2,1)S(1)} %pad_maximum_fusion.4), channel_id=1, source_target_pairs={{0,4},{1,5},{2,6},{3,7},{4,8},{5,9},{6,10},{7,11},{8,12},{9,13},{1... | collective-permute-start | bytes 1179656 | tf_op jit(solution)/shard_map/ppermute | solution.py:248
  7.3 5.2 %collective-permute-done.13.refs_2_ = bf16[96,1152]{1,0:T(8,128)(2,1)S(1)} collective-permute-done((bf16[96,1152]{1,0:T(8,128)(2,1)S(1)}, bf16[96,1152]{1,0:T(8,128)(2,1)S(1)}, u32[]{:S(2)}, u32[]{:S(2)}) %collective-permute-start.13) | collective-permute-done | bytes 221216 | tf_op jit(solution)/shard_map/ppermute | solution.py:249
  12.5 1.3 collective-permute-start.14
  13.8 0.2 collective-permute-start.25
  14.0 5.7 %collective-permute-start.1 = (bf16[8,112,384]{2,1,0:T(8,128)(2,1)S(1)}, bf16[8,112,384]{2,1,0:T(8,128)(2,1)S(1)}, u32[]{:S(2)}, u32[]{:S(2)}) collective-permute-start(bf16[8,112,384]{2,1,0:T(8,128)(2,1)S(1)} %pad_maximum_fusion.2), channel_id=1, source_target_pairs={{1,2},{3,4},{5,6},{7,8},{9,10},{11,12},{13,14},{2,1},{4,3},{6,5},{... | collective-permute-start | bytes 2064392 | tf_op jit(solution)/shard_map/ppermute | solution.py:312
  19.7 1.3 collective-permute-start.5
  21.1 2.1 %collective-permute-done.25 = bf16[96,2048]{1,0:T(8,128)(2,1)S(1)} collective-permute-done((bf16[96,2048]{1,0:T(8,128)(2,1)S(1)}, bf16[96,2048]{1,0:T(8,128)(2,1)S(1)}, u32[]{:S(2)}, u32[]{:S(2)}) %collective-permute-start.25) | collective-permute-done | bytes 393248 | tf_op jit(solution)/shard_map/ppermute | solution.py:249
  23.2 0.1 collective-permute-start.10
  23.4 4.4 %collective-permute-done.14.refs_8_ = bf16[192,1152]{1,0:T(8,128)(2,1)S(1)} collective-permute-done((bf16[192,1152]{1,0:T(8,128)(2,1)S(1)}, bf16[192,1152]{1,0:T(8,128)(2,1)S(1)}, u32[]{:S(2)}, u32[]{:S(2)}) %collective-permute-start.14) | collective-permute-done | bytes 442400 | tf_op jit(solution)/shard_map/ppermute | solution.py:248
  27.8 1.8 %collective-permute-start.29 = (bf16[192,1152]{1,0:T(8,128)(2,1)S(1)}, bf16[192,1152]{1,0:T(8,128)(2,1)S(1)}, u32[]{:S(2)}, u32[]{:S(2)}) collective-permute-start(bf16[192,1152]{1,0:T(8,128)(2,1)S(1)} %collective-permute-done.14.refs_8_), channel_id=1, source_target_pairs={{0,1},{1,0},{2,3},{3,2},{4,5},{5,4},{6,7},{7,6},{8,9},{9,8},{10,11... | collective-permute-start | bytes 1327112 | tf_op jit(solution)/shard_map/ppermute | solution.py:250
  29.7 14.8 %collective-permute-done.5 = bf16[96,2048]{1,0:T(8,128)(2,1)S(1)} collective-permute-done((bf16[96,2048]{1,0:T(8,128)(2,1)S(1)}, bf16[96,2048]{1,0:T(8,128)(2,1)S(1)}, u32[]{:S(2)}, u32[]{:S(2)}) %collective-permute-start.5) | collective-permute-done | bytes 393248 | tf_op jit(solution)/shard_map/ppermute | solution.py:248
  44.4 2.2 %collective-permute-start.15 = (bf16[192,1152]{1,0:T(8,128)(2,1)S(1)}, bf16[192,1152]{1,0:T(8,128)(2,1)S(1)}, u32[]{:S(2)}, u32[]{:S(2)}) collective-permute-start(bf16[192,1152]{1,0:T(8,128)(2,1)S(1)} %collective-permute-done.14.refs_8_), channel_id=1, source_target_pairs={{0,4},{1,5},{2,6},{3,7},{4,8},{5,9},{6,10},{7,11},{8,12},{9,13},{1... | collective-permute-start | bytes 1327112 | tf_op jit(solution)/shard_map/ppermute | solution.py:248
  46.7 1.3 collective-permute-start.27
  48.0 0.2 collective-permute-done.10
  48.1 1.3 collective-permute-start.6
  49.4 2.3 %collective-permute-start.17 = (bf16[96,2048]{1,0:T(8,128)(2,1)S(1)}, bf16[96,2048]{1,0:T(8,128)(2,1)S(1)}, u32[]{:S(2)}, u32[]{:S(2)}) collective-permute-start(bf16[96,2048]{1,0:T(8,128)(2,1)S(1)} %collective-permute-done.5), channel_id=1, source_target_pairs={{0,2},{1,3},{2,0},{3,1},{4,6},{5,7},{6,4},{7,5},{8,10},{9,11},{10,... | collective-permute-start | bytes 1179656 | tf_op jit(solution)/shard_map/ppermute | solution.py:249
  51.8 4.0 %collective-permute-done.15.refs_2_ = bf16[192,1152]{1,0:T(8,128)(2,1)S(1)} collective-permute-done((bf16[192,1152]{1,0:T(8,128)(2,1)S(1)}, bf16[192,1152]{1,0:T(8,128)(2,1)S(1)}, u32[]{:S(2)}, u32[]{:S(2)}) %collective-permute-start.15) | collective-permute-done | bytes 442400 | tf_op jit(solution)/shard_map/ppermute | solution.py:248
  55.8 6.9 %collective-permute-done.6 = bf16[96,2048]{1,0:T(8,128)(2,1)S(1)} collective-permute-done((bf16[96,2048]{1,0:T(8,128)(2,1)S(1)}, bf16[96,2048]{1,0:T(8,128)(2,1)S(1)}, u32[]{:S(2)}, u32[]{:S(2)}) %collective-permute-start.6) | collective-permute-done | bytes 393248 | tf_op jit(solution)/shard_map/ppermute | solution.py:248
  62.9 1.3 collective-permute-start.11
  64.1 0.8 collective-permute-start.28
  64.9 11.7 %collective-permute-done.21.refs_8_ = bf16[192,1152]{1,0:T(8,128)(2,1)S(1)} collective-permute-done((bf16[192,1152]{1,0:T(8,128)(2,1)S(1)}, bf16[192,1152]{1,0:T(8,128)(2,1)S(1)}, u32[]{:S(2)}, u32[]{:S(2)}) %collective-permute-start.21) | collective-permute-done | bytes 442400 | tf_op jit(solution)/shard_map/ppermute | solution.py:248
  76.7 0.4 collective-permute-start.18
  77.0 3.2 %collective-permute-start.7 = (bf16[96,2048]{1,0:T(8,128)(2,1)S(1)}, bf16[96,2048]{1,0:T(8,128)(2,1)S(1)}, u32[]{:S(2)}, u32[]{:S(2)}) collective-permute-start(bf16[96,2048]{1,0:T(8,128)(2,1)S(1)} %collective-permute-done.6), channel_id=1, source_target_pairs={{0,2},{1,3},{2,0},{3,1},{4,6},{5,7},{6,4},{7,5},{8,10},{9,11},{10,... | collective-permute-start | bytes 1179656 | tf_op jit(solution)/shard_map/ppermute | solution.py:249
  80.3 9.4 %collective-permute-done.7.refs_10_ = bf16[96,2048]{1,0:T(8,128)(2,1)S(1)} collective-permute-done((bf16[96,2048]{1,0:T(8,128)(2,1)S(1)}, bf16[96,2048]{1,0:T(8,128)(2,1)S(1)}, u32[]{:S(2)}, u32[]{:S(2)}) %collective-permute-start.7) | collective-permute-done | bytes 393248 | tf_op jit(solution)/shard_map/ppermute | solution.py:249
  89.7 0.8 collective-permute-start.8
  90.5 0.9 collective-permute-start.22
  91.5 6.9 %collective-permute-done.19.refs_6_ = bf16[192,2048]{1,0:T(8,128)(2,1)S(1)} collective-permute-done((bf16[192,2048]{1,0:T(8,128)(2,1)S(1)}, bf16[192,2048]{1,0:T(8,128)(2,1)S(1)}, u32[]{:S(2)}, u32[]{:S(2)}) %collective-permute-start.19) | collective-permute-done | bytes 786464 | tf_op jit(solution)/shard_map/ppermute | solution.py:251
  98.4 2.3 %collective-permute-start.12 = (bf16[192,2048]{1,0:T(8,128)(2,1)S(1)}, bf16[192,2048]{1,0:T(8,128)(2,1)S(1)}, u32[]{:S(2)}, u32[]{:S(2)}) collective-permute-start(bf16[192,2048]{1,0:T(8,128)(2,1)S(1)} %collective-permute-done.11.refs_0_), channel_id=1, source_target_pairs={{0,1},{1,0},{2,3},{3,2},{4,5},{5,4},{6,7},{7,6},{8,9},{9,8},{10,11... | collective-permute-start | bytes 2359304 | tf_op jit(solution)/shard_map/ppermute | solution.py:250
  100.7 6.1 %collective-permute-done.8.refs_0_ = bf16[96,2048]{1,0:T(8,128)(2,1)S(1)} collective-permute-done((bf16[96,2048]{1,0:T(8,128)(2,1)S(1)}, bf16[96,2048]{1,0:T(8,128)(2,1)S(1)}, u32[]{:S(2)}, u32[]{:S(2)}) %collective-permute-start.8) | collective-permute-done | bytes 393248 | tf_op jit(solution)/shard_map/ppermute | solution.py:251
  106.8 1.4 collective-permute-start.9
  108.2 0.2 pad_maximum_fusion
  108.4 0.4 shard_map.113.rows
  108.7 3.2 %shard_map.114 = (bf16[384,10368]{1,0:T(8,128)(2,1)S(1)}, bf16[384,10368]{1,0:T(8,128)(2,1)S(1)}) custom-call(bf16[48,10368]{1,0:T(8,128)(2,1)S(1)} %get-tuple-element.32.refs_0_, bf16[48,10368]{1,0:T(8,128)(2,1)S(1)} %get-tuple-element.33.refs_1_, bf16[96,1152]{1,0:T(8,128)(2,1)S(1)} %collective-permute-done.13.refs_2_, ...), custom_call_target="tpu_custom_call" | custom-call | flops 297271296 | bytes 4194304 | tf_op jit(solution)/shard_map/pallas_call | solution.py:190
  112.0 2.8 %shard_map.115 = (bf16[384,10368]{1,0:T(8,128)(2,1)S(1)}, bf16[384,10368]{1,0:T(8,128)(2,1)S(1)}) custom-call(bf16[192,2048]{1,0:T(8,128)(2,1)S(1)} %collective-permute-done.11.refs_0_, bf16[192,2048]{1,0:T(8,128)(2,1)S(1)} %collective-permute-done.12.refs_1_, ...), custom_call_target="tpu_custom_call", output_to_operand_aliasing={{0}: (12, {}), {1}: (13, {})} | custom-call | flops 297271296 | bytes 4194304 | tf_op jit(solution)/shard_map/pallas_call | solution.py:190
  114.9 5.5 %shard_map.116 = (bf16[2,112,384]{2,1,0:T(8,128)(2,1)S(1)}, bf16[2,112,384]{2,1,0:T(8,128)(2,1)S(1)}, bf16[384,10368]{1,0:T(8,128)(2,1)S(1)}, bf16[384,10368]{1,0:T(8,128)(2,1)S(1)}) custom-call(bf16[3,4,112,384]{3,2,1,0:T(8,128)(2,1)S(1)} %shard_map.113.rows, f32[384]{0:T(512)S(1)} %copy-done.6, ...), custom_call_target="tpu_custom_call", output_to_operand_aliasing={{2}: (5, {}), {3}: (6, {})} | custom-call | flops 1783627776 | bytes 4194304 | tf_op jit(solution)/shard_map/pallas_call | solution.py:190
  120.5 5.8 %collective-permute-start.32 = (bf16[2,112,384]{2,1,0:T(8,128)(2,1)S(1)}, bf16[2,112,384]{2,1,0:T(8,128)(2,1)S(1)}, u32[]{:S(2)}, u32[]{:S(2)}) collective-permute-start(bf16[2,112,384]{2,1,0:T(8,128)(2,1)S(1)} %get-tuple-element.16.act), channel_id=1, source_target_pairs={{1,2},{3,4},{5,6},{7,8},{9,10},{11,12},{13,14},{2,1},{4,3},{6,5},{... | collective-permute-start | bytes 516104 | tf_op jit(solution)/shard_map/ppermute | solution.py:312
  126.3 1.8 %shard_map.117.grad = bf16[2,112,384]{2,1,0:T(8,128)(2,1)S(1)} custom-call(bf16[2,112,384]{2,1,0:T(8,128)(2,1)S(1)} %bitcast.21, bf16[8,112,384]{2,1,0:T(8,128)(2,1)S(1)} %collective-permute-done.near, bf16[8,112,384]{2,1,0:T(8,128)(2,1)S(1)} %collective-permute-done.1.far, bf16[2,112,384]{2,1,0:T(8,128)(2,1)S(1)} %get-tuple-element.17.middle, ...), custom_call_target="tpu_custom_call" | custom-call | flops 891813888 | bytes 4194304 | tf_op jit(solution)/shard_map/pallas_call | solution.py:190
  128.1 2.4 %collective-permute-start.33 = (bf16[2,112,384]{2,1,0:T(8,128)(2,1)S(1)}, bf16[2,112,384]{2,1,0:T(8,128)(2,1)S(1)}, u32[]{:S(2)}, u32[]{:S(2)}) collective-permute-start(bf16[2,112,384]{2,1,0:T(8,128)(2,1)S(1)} %shard_map.117.grad), channel_id=1, source_target_pairs={{0,1},{1,0},{2,3},{3,2},{4,5},{5,4},{6,7},{7,6},{8,9},{9,8},{10,11... | collective-permute-start | bytes 516104 | tf_op jit(solution)/shard_map/ppermute | solution.py:311
  130.6 2.1 %collective-permute-start.34 = (bf16[2,112,384]{2,1,0:T(8,128)(2,1)S(1)}, bf16[2,112,384]{2,1,0:T(8,128)(2,1)S(1)}, u32[]{:S(2)}, u32[]{:S(2)}) collective-permute-start(bf16[2,112,384]{2,1,0:T(8,128)(2,1)S(1)} %shard_map.117.grad), channel_id=1, source_target_pairs={{1,2},{3,4},{5,6},{7,8},{9,10},{11,12},{13,14},{2,1},{4,3},{6,5},{... | collective-permute-start | bytes 516104 | tf_op jit(solution)/shard_map/ppermute | solution.py:312
  132.7 4.6 %shard_map.118 = (bf16[2,112,384]{2,1,0:T(8,128)(2,1)}, f32[3,224,384]{2,1,0:T(8,128)S(1)}) custom-call(bf16[2,112,384]{2,1,0:T(8,128)(2,1)S(1)} %bitcast.26, bf16[2,112,384]{2,1,0:T(8,128)(2,1)S(1)} %get-tuple-element.16.act, bf16[8,112,384]{2,1,0:T(8,128)(2,1)S(1)} %collective-permute-done.near, bf16[8,112,384]{2,1,0:T(8,128)(2,1)S(1)} %collective-permute-done.1.far, ...), custom_call_target="tpu_custom_call" | custom-call | flops 1981808640 | bytes 4194304 | tf_op jit(solution)/shard_map/pallas_call | solution.py:190
  137.3 1.0 collective-permute-done.34.far
  138.3 2.1 %shard_map.119 = bf16[2,112,384]{2,1,0:T(8,128)(2,1)} custom-call(bf16[2,112,384]{2,1,0:T(8,128)(2,1)S(1)} %collective-permute-done.33.near, bf16[2,112,384]{2,1,0:T(8,128)(2,1)S(1)} %collective-permute-done.34.far, bf16[2,112,384]{2,1,0:T(8,128)(2,1)S(1)} %bitcast.19, bf16[2,112,384]{2,1,0:T(8,128)(2,1)S(1)} %bitcast.22, f32[384]{0:T(512)S(1)} %copy-done.5, ...), custom_call_target="tpu_custom_call" | custom-call | flops 594542592 | bytes 4194304 | tf_op jit(solution)/shard_map/pallas_call | solution.py:190
  (60 shorter events, 0.8 us)
Async XLA Ops:
  0.6 2.6 %collective-permute-start.2 = (bf16[24,10368]{1,0:T(8,128)(2,1)}, bf16[24,10368]{1,0:T(8,128)(2,1)S(1)}, u32[]{:S(2)}, u32[]{:S(2)}) collective-permute-start(bf16[24,10368]{1,0:T(8,128)(2,1)} %bitcast.27), channel_id=1, source_target_pairs={{0,1},{1,0},{2,3},{3,2},{4,5},{5,4},{6,7},{7,6},{8,9},{9,8},{10,11... | collective-permute-start | bytes 1493000 | tf_op jit(solution)/shard_map/ppermute | solution.py:250
  1.4 3.0 %collective-permute-start.3 = (bf16[24,10368]{1,0:T(8,128)(2,1)}, bf16[24,10368]{1,0:T(8,128)(2,1)S(1)}, u32[]{:S(2)}, u32[]{:S(2)}) collective-permute-start(bf16[24,10368]{1,0:T(8,128)(2,1)} %bitcast.28), channel_id=1, source_target_pairs={{0,1},{1,0},{2,3},{3,2},{4,5},{5,4},{6,7},{7,6},{8,9},{9,8},{10,11... | collective-permute-start | bytes 1493000 | tf_op jit(solution)/shard_map/ppermute | solution.py:250
  2.7 26.8 %collective-permute-start = (bf16[8,112,384]{2,1,0:T(8,128)(2,1)S(1)}, bf16[8,112,384]{2,1,0:T(8,128)(2,1)S(1)}, u32[]{:S(2)}, u32[]{:S(2)}) collective-permute-start(bf16[8,112,384]{2,1,0:T(8,128)(2,1)S(1)} %pad_maximum_fusion.2), channel_id=1, source_target_pairs={{0,1},{1,0},{2,3},{3,2},{4,5},{5,4},{6,7},{7,6},{8,9},{9,8},{10,11... | collective-permute-start | bytes 2064392 | tf_op jit(solution)/shard_map/ppermute | solution.py:311
  5.5 102.9 %copy-start = (bf16[2,1,112,384]{3,2,1,0:T(8,128)(2,1)S(1)}, bf16[2,1,112,384]{3,2,1,0:T(8,128)(2,1)}, u32[]{:S(2)}) copy-start(bf16[2,1,112,384]{3,2,1,0:T(8,128)(2,1)} %param.10) | copy-start | bytes 516100
  5.5 102.9 %copy-start.2 = (bf16[2,1,112,384]{3,2,1,0:T(8,128)(2,1)S(1)}, bf16[2,1,112,384]{3,2,1,0:T(8,128)(2,1)}, u32[]{:S(2)}) copy-start(bf16[2,1,112,384]{3,2,1,0:T(8,128)(2,1)} %param.11) | copy-start | bytes 516100
  5.5 102.9 %copy-start.5 = (f32[384]{0:T(512)S(1)}, f32[384]{0:T(512)}, u32[]{:S(2)}) copy-start(f32[384]{0:T(512)} %gain.7) | copy-start | bytes 4612
  5.6 6.8 %collective-permute-start.13 = (bf16[96,1152]{1,0:T(8,128)(2,1)S(1)}, bf16[96,1152]{1,0:T(8,128)(2,1)S(1)}, u32[]{:S(2)}, u32[]{:S(2)}) collective-permute-start(bf16[96,1152]{1,0:T(8,128)(2,1)S(1)} %pad_maximum_fusion.5), channel_id=1, source_target_pairs={{0,2},{1,3},{2,0},{3,1},{4,6},{5,7},{6,4},{7,5},{8,10},{9,11},{10,... | collective-permute-start | bytes 663560 | tf_op jit(solution)/shard_map/ppermute | solution.py:249
  5.7 14.0 %collective-permute-start.4 = (bf16[96,2048]{1,0:T(8,128)(2,1)S(1)}, bf16[96,2048]{1,0:T(8,128)(2,1)S(1)}, u32[]{:S(2)}, u32[]{:S(2)}) collective-permute-start(bf16[96,2048]{1,0:T(8,128)(2,1)S(1)} %pad_maximum_fusion.4), channel_id=1, source_target_pairs={{0,4},{1,5},{2,6},{3,7},{4,8},{5,9},{6,10},{7,11},{8,12},{9,13},{1... | collective-permute-start | bytes 1179656 | tf_op jit(solution)/shard_map/ppermute | solution.py:248
  12.5 15.3 %collective-permute-start.14 = (bf16[192,1152]{1,0:T(8,128)(2,1)S(1)}, bf16[192,1152]{1,0:T(8,128)(2,1)S(1)}, u32[]{:S(2)}, u32[]{:S(2)}) collective-permute-start(bf16[192,1152]{1,0:T(8,128)(2,1)S(1)} %pad_maximum_fusion.3), channel_id=1, source_target_pairs={{0,4},{1,5},{2,6},{3,7},{4,8},{5,9},{6,10},{7,11},{8,12},{9,13},{1... | collective-permute-start | bytes 1327112 | tf_op jit(solution)/shard_map/ppermute | solution.py:248
  13.8 9.4 %collective-permute-start.25 = (bf16[96,2048]{1,0:T(8,128)(2,1)S(1)}, bf16[96,2048]{1,0:T(8,128)(2,1)S(1)}, u32[]{:S(2)}, u32[]{:S(2)}) collective-permute-start(bf16[96,2048]{1,0:T(8,128)(2,1)S(1)} %pad_maximum_fusion.4), channel_id=1, source_target_pairs={{0,2},{1,3},{2,0},{3,1},{4,6},{5,7},{6,4},{7,5},{8,10},{9,11},{10,... | collective-permute-start | bytes 1179656 | tf_op jit(solution)/shard_map/ppermute | solution.py:249
  14.0 32.6 %collective-permute-start.1 = (bf16[8,112,384]{2,1,0:T(8,128)(2,1)S(1)}, bf16[8,112,384]{2,1,0:T(8,128)(2,1)S(1)}, u32[]{:S(2)}, u32[]{:S(2)}) collective-permute-start(bf16[8,112,384]{2,1,0:T(8,128)(2,1)S(1)} %pad_maximum_fusion.2), channel_id=1, source_target_pairs={{1,2},{3,4},{5,6},{7,8},{9,10},{11,12},{13,14},{2,1},{4,3},{6,5},{... | collective-permute-start | bytes 2064392 | tf_op jit(solution)/shard_map/ppermute | solution.py:312
  19.7 24.7 %collective-permute-start.5 = (bf16[96,2048]{1,0:T(8,128)(2,1)S(1)}, bf16[96,2048]{1,0:T(8,128)(2,1)S(1)}, u32[]{:S(2)}, u32[]{:S(2)}) collective-permute-start(bf16[96,2048]{1,0:T(8,128)(2,1)S(1)} %collective-permute-done.4), channel_id=1, source_target_pairs={{0,4},{1,5},{2,6},{3,7},{4,8},{5,9},{6,10},{7,11},{8,12},{9,13},{1... | collective-permute-start | bytes 1179656 | tf_op jit(solution)/shard_map/ppermute | solution.py:248
  23.2 24.9 %collective-permute-start.10 = (bf16[96,2048]{1,0:T(8,128)(2,1)S(1)}, bf16[96,2048]{1,0:T(8,128)(2,1)S(1)}, u32[]{:S(2)}, u32[]{:S(2)}) collective-permute-start(bf16[96,2048]{1,0:T(8,128)(2,1)S(1)} %collective-permute-done.4), channel_id=1, source_target_pairs={{0,2},{1,3},{2,0},{3,1},{4,6},{5,7},{6,4},{7,5},{8,10},{9,11},{10,... | collective-permute-start | bytes 1179656 | tf_op jit(solution)/shard_map/ppermute | solution.py:249
  27.8 21.7 %collective-permute-start.29 = (bf16[192,1152]{1,0:T(8,128)(2,1)S(1)}, bf16[192,1152]{1,0:T(8,128)(2,1)S(1)}, u32[]{:S(2)}, u32[]{:S(2)}) collective-permute-start(bf16[192,1152]{1,0:T(8,128)(2,1)S(1)} %collective-permute-done.14.refs_8_), channel_id=1, source_target_pairs={{0,1},{1,0},{2,3},{3,2},{4,5},{5,4},{6,7},{7,6},{8,9},{9,8},{10,11... | collective-permute-start | bytes 1327112 | tf_op jit(solution)/shard_map/ppermute | solution.py:250
  29.6 18.4 %collective-permute-start.24 = (bf16[96,1152]{1,0:T(8,128)(2,1)S(1)}, bf16[96,1152]{1,0:T(8,128)(2,1)S(1)}, u32[]{:S(2)}, u32[]{:S(2)}) collective-permute-start(bf16[96,1152]{1,0:T(8,128)(2,1)S(1)} %collective-permute-done.13.refs_2_), channel_id=1, source_target_pairs={{0,1},{1,0},{2,3},{3,2},{4,5},{5,4},{6,7},{7,6},{8,9},{9,8},{10,11... | collective-permute-start | bytes 663560 | tf_op jit(solution)/shard_map/ppermute | solution.py:250
  44.4 11.4 %collective-permute-start.15 = (bf16[192,1152]{1,0:T(8,128)(2,1)S(1)}, bf16[192,1152]{1,0:T(8,128)(2,1)S(1)}, u32[]{:S(2)}, u32[]{:S(2)}) collective-permute-start(bf16[192,1152]{1,0:T(8,128)(2,1)S(1)} %collective-permute-done.14.refs_8_), channel_id=1, source_target_pairs={{0,4},{1,5},{2,6},{3,7},{4,8},{5,9},{6,10},{7,11},{8,12},{9,13},{1... | collective-permute-start | bytes 1327112 | tf_op jit(solution)/shard_map/ppermute | solution.py:248
  46.7 16.2 %collective-permute-start.27 = (bf16[192,2048]{1,0:T(8,128)(2,1)S(1)}, bf16[192,2048]{1,0:T(8,128)(2,1)S(1)}, u32[]{:S(2)}, u32[]{:S(2)}) collective-permute-start(bf16[192,2048]{1,0:T(8,128)(2,1)S(1)} %constant_dynamic-update-slice_fusion.4.refs_4_), channel_id=1, source_target_pairs={{0,16},{16,0},{1,17},{17,1},{2,18},{18,2},{3,19},{19,3},{4,20},{20... | collective-permute-start | bytes 2359304 | tf_op jit(solution)/shard_map/ppermute | solution.py:251
  47.9 16.2 %collective-permute-start.26 = (bf16[192,2048]{1,0:T(8,128)(2,1)S(1)}, bf16[192,2048]{1,0:T(8,128)(2,1)S(1)}, u32[]{:S(2)}, u32[]{:S(2)}) collective-permute-start(bf16[192,2048]{1,0:T(8,128)(2,1)S(1)} %constant_dynamic-update-slice_fusion.4.refs_4_), channel_id=1, source_target_pairs={{0,1},{1,0},{2,3},{3,2},{4,5},{5,4},{6,7},{7,6},{8,9},{9,8},{10,11... | collective-permute-start | bytes 2359304 | tf_op jit(solution)/shard_map/ppermute | solution.py:250
  48.1 14.6 %collective-permute-start.6 = (bf16[96,2048]{1,0:T(8,128)(2,1)S(1)}, bf16[96,2048]{1,0:T(8,128)(2,1)S(1)}, u32[]{:S(2)}, u32[]{:S(2)}) collective-permute-start(bf16[96,2048]{1,0:T(8,128)(2,1)S(1)} %collective-permute-done.5), channel_id=1, source_target_pairs={{0,4},{1,5},{2,6},{3,7},{4,8},{5,9},{6,10},{7,11},{8,12},{9,13},{1... | collective-permute-start | bytes 1179656 | tf_op jit(solution)/shard_map/ppermute | solution.py:248
  49.4 13.3 %collective-permute-start.17 = (bf16[96,2048]{1,0:T(8,128)(2,1)S(1)}, bf16[96,2048]{1,0:T(8,128)(2,1)S(1)}, u32[]{:S(2)}, u32[]{:S(2)}) collective-permute-start(bf16[96,2048]{1,0:T(8,128)(2,1)S(1)} %collective-permute-done.5), channel_id=1, source_target_pairs={{0,2},{1,3},{2,0},{3,1},{4,6},{5,7},{6,4},{7,5},{8,10},{9,11},{10,... | collective-permute-start | bytes 1179656 | tf_op jit(solution)/shard_map/ppermute | solution.py:249
  55.8 21.2 %collective-permute-start.30 = (bf16[192,2048]{1,0:T(8,128)(2,1)S(1)}, bf16[192,2048]{1,0:T(8,128)(2,1)S(1)}, u32[]{:S(2)}, u32[]{:S(2)}) collective-permute-start(bf16[192,2048]{1,0:T(8,128)(2,1)S(1)} %constant_dynamic-update-slice_fusion.refs_10_), channel_id=1, source_target_pairs={{0,1},{1,0},{2,3},{3,2},{4,5},{5,4},{6,7},{7,6},{8,9},{9,8},{10,11... | collective-permute-start | bytes 2359304 | tf_op jit(solution)/shard_map/ppermute | solution.py:250
  62.8 13.9 %collective-permute-start.21 = (bf16[192,1152]{1,0:T(8,128)(2,1)S(1)}, bf16[192,1152]{1,0:T(8,128)(2,1)S(1)}, u32[]{:S(2)}, u32[]{:S(2)}) collective-permute-start(bf16[192,1152]{1,0:T(8,128)(2,1)S(1)} %collective-permute-done.15.refs_2_), channel_id=1, source_target_pairs={{0,4},{1,5},{2,6},{3,7},{4,8},{5,9},{6,10},{7,11},{8,12},{9,13},{1... | collective-permute-start | bytes 1327112 | tf_op jit(solution)/shard_map/ppermute | solution.py:248
  62.8 13.9 %collective-permute-start.16 = (bf16[192,1152]{1,0:T(8,128)(2,1)S(1)}, bf16[192,1152]{1,0:T(8,128)(2,1)S(1)}, u32[]{:S(2)}, u32[]{:S(2)}) collective-permute-start(bf16[192,1152]{1,0:T(8,128)(2,1)S(1)} %collective-permute-done.15.refs_2_), channel_id=1, source_target_pairs={{0,1},{1,0},{2,3},{3,2},{4,5},{5,4},{6,7},{7,6},{8,9},{9,8},{10,11... | collective-permute-start | bytes 1327112 | tf_op jit(solution)/shard_map/ppermute | solution.py:250
  62.9 27.6 %collective-permute-start.11 = (bf16[192,2048]{1,0:T(8,128)(2,1)S(1)}, bf16[192,2048]{1,0:T(8,128)(2,1)S(1)}, u32[]{:S(2)}, u32[]{:S(2)}) collective-permute-start(bf16[192,2048]{1,0:T(8,128)(2,1)S(1)} %constant_dynamic-update-slice_fusion.refs_10_), channel_id=1, source_target_pairs={{0,16},{16,0},{1,17},{17,1},{2,18},{18,2},{3,19},{19,3},{4,20},{20... | collective-permute-start | bytes 2359304 | tf_op jit(solution)/shard_map/ppermute | solution.py:251
  64.1 27.2 %collective-permute-start.28 = (bf16[192,2048]{1,0:T(8,128)(2,1)S(1)}, bf16[192,2048]{1,0:T(8,128)(2,1)S(1)}, u32[]{:S(2)}, u32[]{:S(2)}) collective-permute-start(bf16[192,2048]{1,0:T(8,128)(2,1)S(1)} %collective-permute-done.27.refs_6_), channel_id=1, source_target_pairs={{0,1},{1,0},{2,3},{3,2},{4,5},{5,4},{6,7},{7,6},{8,9},{9,8},{10,11... | collective-permute-start | bytes 2359304 | tf_op jit(solution)/shard_map/ppermute | solution.py:250
  76.6 21.8 %collective-permute-start.19 = (bf16[192,2048]{1,0:T(8,128)(2,1)S(1)}, bf16[192,2048]{1,0:T(8,128)(2,1)S(1)}, u32[]{:S(2)}, u32[]{:S(2)}) collective-permute-start(bf16[192,2048]{1,0:T(8,128)(2,1)S(1)} %constant_dynamic-update-slice_fusion.2.refs_4_), channel_id=1, source_target_pairs={{0,16},{16,0},{1,17},{17,1},{2,18},{18,2},{3,19},{19,3},{4,20},{20... | collective-permute-start | bytes 2359304 | tf_op jit(solution)/shard_map/ppermute | solution.py:251
  76.7 24.0 %collective-permute-start.18 = (bf16[192,2048]{1,0:T(8,128)(2,1)S(1)}, bf16[192,2048]{1,0:T(8,128)(2,1)S(1)}, u32[]{:S(2)}, u32[]{:S(2)}) collective-permute-start(bf16[192,2048]{1,0:T(8,128)(2,1)S(1)} %constant_dynamic-update-slice_fusion.2.refs_4_), channel_id=1, source_target_pairs={{0,1},{1,0},{2,3},{3,2},{4,5},{5,4},{6,7},{7,6},{8,9},{9,8},{10,11... | collective-permute-start | bytes 2359304 | tf_op jit(solution)/shard_map/ppermute | solution.py:250
  77.0 12.7 %collective-permute-start.7 = (bf16[96,2048]{1,0:T(8,128)(2,1)S(1)}, bf16[96,2048]{1,0:T(8,128)(2,1)S(1)}, u32[]{:S(2)}, u32[]{:S(2)}) collective-permute-start(bf16[96,2048]{1,0:T(8,128)(2,1)S(1)} %collective-permute-done.6), channel_id=1, source_target_pairs={{0,2},{1,3},{2,0},{3,1},{4,6},{5,7},{6,4},{7,5},{8,10},{9,11},{10,... | collective-permute-start | bytes 1179656 | tf_op jit(solution)/shard_map/ppermute | solution.py:249
  89.7 17.1 %collective-permute-start.8 = (bf16[96,2048]{1,0:T(8,128)(2,1)S(1)}, bf16[96,2048]{1,0:T(8,128)(2,1)S(1)}, u32[]{:S(2)}, u32[]{:S(2)}) collective-permute-start(bf16[96,2048]{1,0:T(8,128)(2,1)S(1)} %collective-permute-done.7.refs_10_), channel_id=1, source_target_pairs={{0,16},{16,0},{1,17},{17,1},{2,18},{18,2},{3,19},{19,3},{4,20},{20... | collective-permute-start | bytes 1179656 | tf_op jit(solution)/shard_map/ppermute | solution.py:251
  90.5 21.5 %collective-permute-start.22 = (bf16[192,1152]{1,0:T(8,128)(2,1)S(1)}, bf16[192,1152]{1,0:T(8,128)(2,1)S(1)}, u32[]{:S(2)}, u32[]{:S(2)}) collective-permute-start(bf16[192,1152]{1,0:T(8,128)(2,1)S(1)} %collective-permute-done.21.refs_8_), channel_id=1, source_target_pairs={{0,1},{1,0},{2,3},{3,2},{4,5},{5,4},{6,7},{7,6},{8,9},{9,8},{10,11... | collective-permute-start | bytes 1327112 | tf_op jit(solution)/shard_map/ppermute | solution.py:250
  91.4 20.6 %collective-permute-start.23 = (bf16[96,2048]{1,0:T(8,128)(2,1)S(1)}, bf16[96,2048]{1,0:T(8,128)(2,1)S(1)}, u32[]{:S(2)}, u32[]{:S(2)}) collective-permute-start(bf16[96,2048]{1,0:T(8,128)(2,1)S(1)} %collective-permute-done.7.refs_10_), channel_id=1, source_target_pairs={{0,1},{1,0},{2,3},{3,2},{4,5},{5,4},{6,7},{7,6},{8,9},{9,8},{10,11... | collective-permute-start | bytes 1179656 | tf_op jit(solution)/shard_map/ppermute | solution.py:250
  98.4 13.6 %collective-permute-start.12 = (bf16[192,2048]{1,0:T(8,128)(2,1)S(1)}, bf16[192,2048]{1,0:T(8,128)(2,1)S(1)}, u32[]{:S(2)}, u32[]{:S(2)}) collective-permute-start(bf16[192,2048]{1,0:T(8,128)(2,1)S(1)} %collective-permute-done.11.refs_0_), channel_id=1, source_target_pairs={{0,1},{1,0},{2,3},{3,2},{4,5},{5,4},{6,7},{7,6},{8,9},{9,8},{10,11... | collective-permute-start | bytes 2359304 | tf_op jit(solution)/shard_map/ppermute | solution.py:250
  100.7 11.3 %collective-permute-start.20 = (bf16[192,2048]{1,0:T(8,128)(2,1)S(1)}, bf16[192,2048]{1,0:T(8,128)(2,1)S(1)}, u32[]{:S(2)}, u32[]{:S(2)}) collective-permute-start(bf16[192,2048]{1,0:T(8,128)(2,1)S(1)} %collective-permute-done.19.refs_6_), channel_id=1, source_target_pairs={{0,1},{1,0},{2,3},{3,2},{4,5},{5,4},{6,7},{7,6},{8,9},{9,8},{10,11... | collective-permute-start | bytes 2359304 | tf_op jit(solution)/shard_map/ppermute | solution.py:250
  106.8 8.1 %collective-permute-start.9 = (bf16[96,2048]{1,0:T(8,128)(2,1)S(1)}, bf16[96,2048]{1,0:T(8,128)(2,1)S(1)}, u32[]{:S(2)}, u32[]{:S(2)}) collective-permute-start(bf16[96,2048]{1,0:T(8,128)(2,1)S(1)} %collective-permute-done.8.refs_0_), channel_id=1, source_target_pairs={{0,1},{1,0},{2,3},{3,2},{4,5},{5,4},{6,7},{7,6},{8,9},{9,8},{10,11... | collective-permute-start | bytes 1179656 | tf_op jit(solution)/shard_map/ppermute | solution.py:250
  112.0 2.9 %copy-start.4 = (f32[384]{0:T(512)S(1)}, f32[384]{0:T(512)}, u32[]{:S(2)}) copy-start(f32[384]{0:T(512)} %gain.6) | copy-start | bytes 4612
  112.0 2.9 %copy-start.6 = (f32[384]{0:T(512)S(1)}, f32[384]{0:T(512)}, u32[]{:S(2)}) copy-start(f32[384]{0:T(512)} %bias.2) | copy-start | bytes 4612
  114.9 11.4 %copy-start.1 = (bf16[2,1,112,384]{3,2,1,0:T(8,128)(2,1)S(1)}, bf16[2,1,112,384]{3,2,1,0:T(8,128)(2,1)}, u32[]{:S(2)}) copy-start(bf16[2,1,112,384]{3,2,1,0:T(8,128)(2,1)} %param.19) | copy-start | bytes 516100
  120.4 12.3 %copy-start.3 = (bf16[2,1,112,384]{3,2,1,0:T(8,128)(2,1)S(1)}, bf16[2,1,112,384]{3,2,1,0:T(8,128)(2,1)}, u32[]{:S(2)}) copy-start(bf16[2,1,112,384]{3,2,1,0:T(8,128)(2,1)} %param.12) | copy-start | bytes 516100
  120.4 12.3 %copy-start.7 = (f32[384]{0:T(512)S(1)}, f32[384]{0:T(512)}, u32[]{:S(2)}) copy-start(f32[384]{0:T(512)} %bias.3) | copy-start | bytes 4612
  120.4 12.2 %collective-permute-start.31 = (bf16[2,112,384]{2,1,0:T(8,128)(2,1)S(1)}, bf16[2,112,384]{2,1,0:T(8,128)(2,1)S(1)}, u32[]{:S(2)}, u32[]{:S(2)}) collective-permute-start(bf16[2,112,384]{2,1,0:T(8,128)(2,1)S(1)} %get-tuple-element.16.act), channel_id=1, source_target_pairs={{0,1},{1,0},{2,3},{3,2},{4,5},{5,4},{6,7},{7,6},{8,9},{9,8},{10,11... | collective-permute-start | bytes 516104 | tf_op jit(solution)/shard_map/ppermute | solution.py:311
  120.5 12.2 %collective-permute-start.32 = (bf16[2,112,384]{2,1,0:T(8,128)(2,1)S(1)}, bf16[2,112,384]{2,1,0:T(8,128)(2,1)S(1)}, u32[]{:S(2)}, u32[]{:S(2)}) collective-permute-start(bf16[2,112,384]{2,1,0:T(8,128)(2,1)S(1)} %get-tuple-element.16.act), channel_id=1, source_target_pairs={{1,2},{3,4},{5,6},{7,8},{9,10},{11,12},{13,14},{2,1},{4,3},{6,5},{... | collective-permute-start | bytes 516104 | tf_op jit(solution)/shard_map/ppermute | solution.py:312
  128.1 9.2 %collective-permute-start.33 = (bf16[2,112,384]{2,1,0:T(8,128)(2,1)S(1)}, bf16[2,112,384]{2,1,0:T(8,128)(2,1)S(1)}, u32[]{:S(2)}, u32[]{:S(2)}) collective-permute-start(bf16[2,112,384]{2,1,0:T(8,128)(2,1)S(1)} %shard_map.117.grad), channel_id=1, source_target_pairs={{0,1},{1,0},{2,3},{3,2},{4,5},{5,4},{6,7},{7,6},{8,9},{9,8},{10,11... | collective-permute-start | bytes 516104 | tf_op jit(solution)/shard_map/ppermute | solution.py:311
  130.6 7.7 %collective-permute-start.34 = (bf16[2,112,384]{2,1,0:T(8,128)(2,1)S(1)}, bf16[2,112,384]{2,1,0:T(8,128)(2,1)S(1)}, u32[]{:S(2)}, u32[]{:S(2)}) collective-permute-start(bf16[2,112,384]{2,1,0:T(8,128)(2,1)S(1)} %shard_map.117.grad), channel_id=1, source_target_pairs={{1,2},{3,4},{5,6},{7,8},{9,10},{11,12},{13,14},{2,1},{4,3},{6,5},{... | collective-permute-start | bytes 516104 | tf_op jit(solution)/shard_map/ppermute | solution.py:312

commit v2 on v1

--- a/solution.py
+++ b/solution.py
@@ -10,8 +10,6 @@
 
 TILES = 81
 SOLE = 32
-HALF = SOLE // 2
-MID = (TILES - 2 * SOLE + 1) // 2
 VMEM_LIMIT = 12 * 1024 * 1024
 
 
@@ -216,21 +214,15 @@
             begin = sum(b[3] for b in blocks[:at])
             part = pl.ds(begin, height)
             if kind == "own":
-                column, span, skip = 0, TILES, 0
-            elif kind == "middle" and not crossed:
-                column, span, skip = SOLE + (MID - 1) * whose, MID, 0
+                column, span = 0, TILES
             elif kind == "middle":
-                column, span, skip = SOLE + MID * whose, MID - 1, whose
+                column, span = SOLE * width, TILES - 2 * SOLE
             else:
                 where = 1 - pair if kind == "passed" else pair
-                column, span, skip = (TILES - SOLE) * where + HALF * whose, HALF, 0
-            if not isinstance(skip, int):
-                skip = pl.multiple_of(skip * width, 128)
-            if not isinstance(column, int):
-                column = pl.multiple_of(column * width, 128)
-            row = pl.multiple_of(chip * height, height)
+                column, span = pl.multiple_of((TILES - SOLE) * width * where, 128), SOLE
+            row = pl.multiple_of((2 * chip + whose) * height, height)
             found.append(
-                (source.at[part, pl.ds(skip, span * width)], row, column, height, span * width)
+                (source.at[part], row, column, height, span * width)
             )
     return found
 
@@ -238,33 +230,25 @@
 def gather(shards):
     count, groups = lax.axis_size("ha"), lax.axis_size("grp")
     rows, wide = shards[0].shape
-    if count % 4 or groups % 2 or (2 * rows) % 16:
+    if count % 4 or groups % 2 or rows % 8:
         whole = [lax.all_gather(shard, "ha", axis=0, tiled=True) for shard in shards]
         return whole, [None, None], 0, [0, 0]
     ring = count // 4
     width = wide // TILES
-    chip = 2 * rows
 
     turn = lambda a: lax.ppermute(a, "ha", [(i, (i + 4) % count) for i in range(count)])
     side = lambda a: lax.ppermute(a, "ha", [(i, i ^ 2) for i in range(count)])
     cross = lambda a: lax.ppermute(a, "ha", [(i, i ^ 1) for i in range(count)])
     over = lambda a: lax.ppermute(a, "grp", [(i, i ^ 1) for i in range(groups)])
-    core = lax.axis_index("ha") % 2
     pair = lax.axis_index("grp") % 2
-    others = [cross(shard) for shard in shards]
-
-    own = [
-        jnp.concatenate([jnp.where(core == 0, a, b), jnp.where(core == 0, b, a)], axis=0)
-        for a, b in zip(shards, others)
-    ]
-
-    def chosen(start, taps):
-        return jnp.concatenate(
-            [lax.dynamic_slice_in_dim(o, start * width, taps * width, axis=1) for o in own], axis=0
-        )
-
-    ends = chosen((TILES - SOLE) * pair + HALF * core, HALF)
-    mids = chosen(SOLE + (MID - 1) * core, MID)
+    ends = jnp.concatenate(
+        [
+            lax.dynamic_slice_in_dim(v, (TILES - SOLE) * pair * width, SOLE * width, axis=1)
+            for v in shards
+        ],
+        axis=0,
+    )
+    mids = jnp.concatenate([v[:, SOLE * width : (TILES - SOLE) * width] for v in shards], axis=0)
     arrays, pieces, stages = [], [], []
 
     def keep(array, blocks, kind, stage):
@@ -278,17 +262,15 @@
     ends_next = turn(ends)
     mids_across = side(mids)
     for conv in range(2):
-        arrays.append(own[conv])
-        pieces.append(([(conv, 0, False, chip)], "own", False))
-        stages.append(0)
-    keep(mids_across, [(0, 0, True, chip), (1, 0, True, chip)], "middle", 0)
+        keep(shards[conv], [(conv, 0, False, rows)], "own", 0)
+    keep(mids_across, [(0, 0, True, rows), (1, 0, True, rows)], "middle", 0)
     mids = jnp.concatenate([mids, mids_across], axis=0)
     for step in range(1, ring + 1):
-        blocks = [(0, step - 1, True, chip), (1, step - 1, True, chip)]
+        blocks = [(0, step - 1, True, rows), (1, step - 1, True, rows)]
         both = ends_across
         if step < ring:
             ends = ends_next
-            blocks = [(0, step, False, chip), (1, step, False, chip)] + blocks
+            blocks = [(0, step, False, rows), (1, step, False, rows)] + blocks
             both = jnp.concatenate([ends, ends_across], axis=0)
         keep(both, blocks, "ends", step)
         keep(over(both), blocks, "passed", step + 1)
@@ -297,9 +279,9 @@
             if step + 1 < ring:
                 ends_next = turn(ends)
             mids = turn(mids)
-            chips = [(conv, step, flip, chip) for flip in (False, True) for conv in range(2)]
+            chips = [(conv, step, flip, rows) for flip in (False, True) for conv in range(2)]
             keep(mids, chips, "middle", step + 1)
-    groups = [(stage > ring // 2) + (stage > ring) for stage in stages]
+    groups = [(stage >= ring) + (stage > ring) for stage in stages]
     return arrays, pieces, ring, groups
 
 

time: 143 us -> 150 us (1.049); the launches traced: 140 us -> 149 us
  waiting for transfers between devices: 72.8 us -> 78.8 us
  Pallas kernels: 20.4 us -> 25 us
  local copies, waits for them, and re-layouts: 0.21 us -> 4.02 us
  starting transfers between devices: 42.1 us -> 39.1 us
  other arithmetic: 3.83 us -> 1.36 us
    ppermute x4, waiting for transfers between devices: 13 us -> 22.7 us  [gather(): over = lambda a: lax.ppermute(a, 'grp', [(i, i ^ 1) for i in range(groups)])]
    ppermute x14, starting transfers between devices: 8.48 us -> 14.8 us  [gather(): cross = lambda a: lax.ppermute(a, 'ha', [(i, i ^ 1) for i in range(count)])]
    pallas_call x7, Pallas kernels: 20.4 us -> 25 us  [call(): pl.pallas_call(body, out_shape=outs, in_specs=specs, out_specs=[spec] * l...]
    ppermute x3, starting transfers between devices: 13.5 us -> 10.2 us  [neighbours(): far = lax.ppermute(block, 'ha', outer)]
    ppermute x6, starting transfers between devices: 7.75 us -> 4.61 us  [gather(): lax.ppermute(a, 'ha', [(i, (i + 4) % count) for i in range(count)])]
    ppermute x5, starting transfers between devices: 6.01 us -> 2.91 us  [gather(): side = lambda a: lax.ppermute(a, 'ha', [(i, i ^ 2) for i in range(count)])]
    ppermute x5, waiting for transfers between devices: 16.9 us -> 14.5 us  [gather(): side = lambda a: lax.ppermute(a, 'ha', [(i, i ^ 2) for i in range(count)])]
    select_n x2 -> x0, other arithmetic: 2.21 us -> none  [gather(): jnp.where(core == 0, b, a)]
  transfers between devices with their start and end apart: 35 -> 35, of which waited for: 12 -> 11; matrix products, arithmetic and copies ran while one was open for 3% -> 2% of each run, Pallas kernels for 9% -> 11%
where the time goes in v2:
time: 150 us; the launch traced here: 149 us
  waiting for transfers between devices  78.8 us (53%)
  starting transfers between devices  39.1 us (26%)
  Pallas kernels  25 us (17%)
  local copies, waits for them, and re-layouts  4.02 us (3%)
    ppermute x6, waiting for transfers between devices, gather(): lax.ppermute(a, 'ha', [(i, (i + 4) % count) for i in range(count)])  39.8 us
    pallas_call x7, Pallas kernels, call(): pl.pallas_call(body, out_shape=outs, in_specs=specs, out_specs=[spec] * l...  25 us
    ppermute x4, waiting for transfers between devices, gather(): over = lambda a: lax.ppermute(a, 'grp', [(i, i ^ 1) for i in range(groups)])  22.7 us
    ppermute x14, starting transfers between devices, gather(): cross = lambda a: lax.ppermute(a, 'ha', [(i, i ^ 1) for i in range(count)])  14.8 us
    ppermute x5, waiting for transfers between devices, gather(): side = lambda a: lax.ppermute(a, 'ha', [(i, i ^ 2) for i in range(count)])  14.5 us
    ppermute x3, starting transfers between devices, neighbours(): far = lax.ppermute(block, 'ha', outer)  10.2 us
    ppermute x4, starting transfers between devices, gather(): over = lambda a: lax.ppermute(a, 'grp', [(i, i ^ 1) for i in range(groups)])  4.98 us
    ppermute x6, starting transfers between devices, gather(): lax.ppermute(a, 'ha', [(i, (i + 4) % count) for i in range(count)])  4.61 us
  transfers between devices with their start and end apart: 35, of which 11 were waited for; matrix products, arithmetic and copies ran while one was open for 2% of the time, Pallas kernels for 11%

profile of v2, /device:TPU:5, one launch (start us, length us, event | category | flops | bytes accessed | tf_op | source)
XLA Modules:
  0.0 149.3 jit_solution(182981432757007025)
XLA Ops:
  0.7 1.0 slice.8
  1.7 0.9 slice.9
  2.7 0.9 dynamic-slice_bitcast_fusion
  3.7 0.9 dynamic-slice_bitcast_fusion.1
  4.6 1.5 %collective-permute-start.2 = (bf16[48,4096]{1,0:T(8,128)(2,1)S(1)}, bf16[48,4096]{1,0:T(8,128)(2,1)S(1)}, u32[]{:S(2)}, u32[]{:S(2)}) collective-permute-start(bf16[48,4096]{1,0:T(8,128)(2,1)S(1)} %pad_maximum_fusion.2), channel_id=1, source_target_pairs={{0,4},{1,5},{2,6},{3,7},{4,8},{5,9},{6,10},{7,11},{8,12},{9,13},{1... | collective-permute-start | bytes 1179656 | tf_op jit(solution)/shard_map/ppermute | solution.py:239
  6.2 1.2 collective-permute-start.20
  7.4 1.5 %collective-permute-start.17 = (bf16[24,10368]{1,0:T(8,128)(2,1)}, bf16[24,10368]{1,0:T(8,128)(2,1)S(1)}, u32[]{:S(2)}, u32[]{:S(2)}) collective-permute-start(bf16[24,10368]{1,0:T(8,128)(2,1)} %bitcast.27), channel_id=1, source_target_pairs={{0,1},{1,0},{2,3},{3,2},{4,5},{5,4},{6,7},{7,6},{8,9},{9,8},{10,11... | collective-permute-start | bytes 1493000 | tf_op jit(solution)/shard_map/ppermute | solution.py:241
  8.9 1.3 pad_maximum_fusion
  10.2 1.0 collective-permute-start
  11.3 5.5 %collective-permute-done.2 = bf16[48,4096]{1,0:T(8,128)(2,1)S(1)} collective-permute-done((bf16[48,4096]{1,0:T(8,128)(2,1)S(1)}, bf16[48,4096]{1,0:T(8,128)(2,1)S(1)}, u32[]{:S(2)}, u32[]{:S(2)}) %collective-permute-start.2) | collective-permute-done | bytes 393248 | tf_op jit(solution)/shard_map/ppermute | solution.py:239
  16.7 1.5 %collective-permute-start.19 = (bf16[48,2176]{1,0:T(8,128)(2,1)S(1)}, bf16[48,2176]{1,0:T(8,128)(2,1)S(1)}, u32[]{:S(2)}, u32[]{:S(2)}) collective-permute-start(bf16[48,2176]{1,0:T(8,128)(2,1)S(1)} %collective-permute-done.11.refs_4_), channel_id=1, source_target_pairs={{0,1},{1,0},{2,3},{3,2},{4,5},{5,4},{6,7},{7,6},{8,9},{9,8},{10,11... | collective-permute-start | bytes 626696 | tf_op jit(solution)/shard_map/ppermute | solution.py:241
  18.3 0.3 collective-permute-start.3
  18.6 0.7 collective-permute-done.19.refs_5_
  19.4 4.0 %collective-permute-start.1 = (bf16[8,112,384]{2,1,0:T(8,128)(2,1)S(1)}, bf16[8,112,384]{2,1,0:T(8,128)(2,1)S(1)}, u32[]{:S(2)}, u32[]{:S(2)}) collective-permute-start(bf16[8,112,384]{2,1,0:T(8,128)(2,1)S(1)} %pad_maximum_fusion), channel_id=1, source_target_pairs={{1,2},{3,4},{5,6},{7,8},{9,10},{11,12},{13,14},{2,1},{4,3},{6,5},{... | collective-permute-start | bytes 2064392 | tf_op jit(solution)/shard_map/ppermute | solution.py:294
  23.4 7.1 %collective-permute-done.3 = bf16[48,4096]{1,0:T(8,128)(2,1)S(1)} collective-permute-done((bf16[48,4096]{1,0:T(8,128)(2,1)S(1)}, bf16[48,4096]{1,0:T(8,128)(2,1)S(1)}, u32[]{:S(2)}, u32[]{:S(2)}) %collective-permute-start.3) | collective-permute-done | bytes 393248 | tf_op jit(solution)/shard_map/ppermute | solution.py:239
  30.5 1.6 %collective-permute-start.25 = (bf16[48,4096]{1,0:T(8,128)(2,1)S(1)}, bf16[48,4096]{1,0:T(8,128)(2,1)S(1)}, u32[]{:S(2)}, u32[]{:S(2)}) collective-permute-start(bf16[48,4096]{1,0:T(8,128)(2,1)S(1)} %collective-permute-done.2), channel_id=1, source_target_pairs={{0,2},{1,3},{2,0},{3,1},{4,6},{5,7},{6,4},{7,5},{8,10},{9,11},{10,... | collective-permute-start | bytes 1179656 | tf_op jit(solution)/shard_map/ppermute | solution.py:240
  32.2 1.3 collective-permute-start.22
  33.5 14.4 %collective-permute-done.25 = bf16[48,4096]{1,0:T(8,128)(2,1)S(1)} collective-permute-done((bf16[48,4096]{1,0:T(8,128)(2,1)S(1)}, bf16[48,4096]{1,0:T(8,128)(2,1)S(1)}, u32[]{:S(2)}, u32[]{:S(2)}) %collective-permute-start.25) | collective-permute-done | bytes 393248 | tf_op jit(solution)/shard_map/ppermute | solution.py:240
  48.0 1.3 collective-permute-start.4
  49.4 1.3 collective-permute-start.13
  50.7 0.7 collective-permute-start.24
  51.5 8.5 %collective-permute-done.4 = bf16[48,4096]{1,0:T(8,128)(2,1)S(1)} collective-permute-done((bf16[48,4096]{1,0:T(8,128)(2,1)S(1)}, bf16[48,4096]{1,0:T(8,128)(2,1)S(1)}, u32[]{:S(2)}, u32[]{:S(2)}) %collective-permute-start.4) | collective-permute-done | bytes 393248 | tf_op jit(solution)/shard_map/ppermute | solution.py:239
  60.0 8.9 %collective-permute-done.13.refs_16_ = bf16[96,2176]{1,0:T(8,128)(2,1)S(1)} collective-permute-done((bf16[96,2176]{1,0:T(8,128)(2,1)S(1)}, bf16[96,2176]{1,0:T(8,128)(2,1)S(1)}, u32[]{:S(2)}, u32[]{:S(2)}) %collective-permute-start.13) | collective-permute-done | bytes 417824 | tf_op jit(solution)/shard_map/ppermute | solution.py:239
  68.9 1.2 collective-permute-start.27
  70.1 1.6 %collective-permute-start.26 = (bf16[96,4096]{1,0:T(8,128)(2,1)S(1)}, bf16[96,4096]{1,0:T(8,128)(2,1)S(1)}, u32[]{:S(2)}, u32[]{:S(2)}) collective-permute-start(bf16[96,4096]{1,0:T(8,128)(2,1)S(1)} %constant_dynamic-update-slice_fusion.4.refs_12_), channel_id=1, source_target_pairs={{0,1},{1,0},{2,3},{3,2},{4,5},{5,4},{6,7},{7,6},{8,9},{9,8},{10,11... | collective-permute-start | bytes 2359304 | tf_op jit(solution)/shard_map/ppermute | solution.py:241
  71.9 1.3 collective-permute-start.9
  73.2 1.0 collective-permute-done.29.refs_17_
  74.2 0.4 collective-permute-start.30
  74.6 9.7 %collective-permute-done.14.refs_2_ = bf16[96,2176]{1,0:T(8,128)(2,1)S(1)} collective-permute-done((bf16[96,2176]{1,0:T(8,128)(2,1)S(1)}, bf16[96,2176]{1,0:T(8,128)(2,1)S(1)}, u32[]{:S(2)}, u32[]{:S(2)}) %collective-permute-start.14) | collective-permute-done | bytes 417824 | tf_op jit(solution)/shard_map/ppermute | solution.py:239
  84.4 1.3 collective-permute-start.23
  85.7 1.0 collective-permute-done.27.refs_14_
  86.7 4.0 %collective-permute-start.28 = (bf16[96,4096]{1,0:T(8,128)(2,1)S(1)}, bf16[96,4096]{1,0:T(8,128)(2,1)S(1)}, u32[]{:S(2)}, u32[]{:S(2)}) collective-permute-start(bf16[96,4096]{1,0:T(8,128)(2,1)S(1)} %collective-permute-done.27.refs_14_), channel_id=1, source_target_pairs={{0,1},{1,0},{2,3},{3,2},{4,5},{5,4},{6,7},{7,6},{8,9},{9,8},{10,11... | collective-permute-start | bytes 2359304 | tf_op jit(solution)/shard_map/ppermute | solution.py:241
  90.7 12.8 %collective-permute-done.9.refs_0_ = bf16[96,4096]{1,0:T(8,128)(2,1)S(1)} collective-permute-done((bf16[96,4096]{1,0:T(8,128)(2,1)S(1)}, bf16[96,4096]{1,0:T(8,128)(2,1)S(1)}, u32[]{:S(2)}, u32[]{:S(2)}) %collective-permute-start.9) | collective-permute-done | bytes 786464 | tf_op jit(solution)/shard_map/ppermute | solution.py:242
  103.5 2.2 %collective-permute-start.10 = (bf16[96,4096]{1,0:T(8,128)(2,1)S(1)}, bf16[96,4096]{1,0:T(8,128)(2,1)S(1)}, u32[]{:S(2)}, u32[]{:S(2)}) collective-permute-start(bf16[96,4096]{1,0:T(8,128)(2,1)S(1)} %collective-permute-done.9.refs_0_), channel_id=1, source_target_pairs={{0,1},{1,0},{2,3},{3,2},{4,5},{5,4},{6,7},{7,6},{8,9},{9,8},{10,11... | collective-permute-start | bytes 2359304 | tf_op jit(solution)/shard_map/ppermute | solution.py:241
  105.7 1.2 collective-permute-start.6
  106.9 0.3 collective-permute-start.15
  107.4 8.9 %collective-permute-done.6.refs_0_ = bf16[48,4096]{1,0:T(8,128)(2,1)S(1)} collective-permute-done((bf16[48,4096]{1,0:T(8,128)(2,1)S(1)}, bf16[48,4096]{1,0:T(8,128)(2,1)S(1)}, u32[]{:S(2)}, u32[]{:S(2)}) %collective-permute-start.6) | collective-permute-done | bytes 393248 | tf_op jit(solution)/shard_map/ppermute | solution.py:242
  116.4 0.9 collective-permute-start.7
  117.2 0.4 shard_map.113.rows
  117.6 8.4 %shard_map.114 = (bf16[384,10368]{1,0:T(8,128)(2,1)S(1)}, bf16[384,10368]{1,0:T(8,128)(2,1)S(1)}) custom-call(bf16[24,10368]{1,0:T(8,128)(2,1)S(1)} %bitcast.28, bf16[24,10368]{1,0:T(8,128)(2,1)S(1)} %collective-permute-done.17.refs_1_, bf16[24,10368]{1,0:T(8,128)(2,1)S(1)} %bitcast.25, bf16[24,10368]{1,0:T(8,128)(2,1)S(1)} %collective-permute-done.18.refs_3_, ...), custom_call_target="tpu_custom_call" | custom-call | flops 297271296 | bytes 4194304 | tf_op jit(solution)/shard_map/pallas_call | solution.py:188
  126.1 1.9 %shard_map.115 = (bf16[384,10368]{1,0:T(8,128)(2,1)S(1)}, bf16[384,10368]{1,0:T(8,128)(2,1)S(1)}) custom-call(bf16[96,4096]{1,0:T(8,128)(2,1)S(1)} %collective-permute-done.9.refs_0_, bf16[96,4096]{1,0:T(8,128)(2,1)S(1)} %collective-permute-done.10.refs_1_, ...), custom_call_target="tpu_custom_call", output_to_operand_aliasing={{0}: (6, {}), {1}: (7, {})} | custom-call | flops 297271296 | bytes 4194304 | tf_op jit(solution)/shard_map/pallas_call | solution.py:188
  128.1 5.8 %shard_map.116 = (bf16[2,112,384]{2,1,0:T(8,128)(2,1)S(1)}, bf16[2,112,384]{2,1,0:T(8,128)(2,1)S(1)}, bf16[384,10368]{1,0:T(8,128)(2,1)S(1)}, bf16[384,10368]{1,0:T(8,128)(2,1)S(1)}) custom-call(bf16[3,4,112,384]{3,2,1,0:T(8,128)(2,1)S(1)} %shard_map.113.rows, f32[384]{0:T(512)S(1)} %copy-done.8, ...), custom_call_target="tpu_custom_call", output_to_operand_aliasing={{2}: (5, {}), {3}: (6, {})} | custom-call | flops 1783627776 | bytes 4194304 | tf_op jit(solution)/shard_map/pallas_call | solution.py:188
  134.0 1.9 %collective-permute-start.32 = (bf16[2,112,384]{2,1,0:T(8,128)(2,1)S(1)}, bf16[2,112,384]{2,1,0:T(8,128)(2,1)S(1)}, u32[]{:S(2)}, u32[]{:S(2)}) collective-permute-start(bf16[2,112,384]{2,1,0:T(8,128)(2,1)S(1)} %get-tuple-element.16.act), channel_id=1, source_target_pairs={{1,2},{3,4},{5,6},{7,8},{9,10},{11,12},{13,14},{2,1},{4,3},{6,5},{... | collective-permute-start | bytes 516104 | tf_op jit(solution)/shard_map/ppermute | solution.py:294
  135.9 1.9 %shard_map.117.grad = bf16[2,112,384]{2,1,0:T(8,128)(2,1)S(1)} custom-call(bf16[2,112,384]{2,1,0:T(8,128)(2,1)S(1)} %bitcast.21, bf16[8,112,384]{2,1,0:T(8,128)(2,1)S(1)} %collective-permute-done.near, bf16[8,112,384]{2,1,0:T(8,128)(2,1)S(1)} %collective-permute-done.1.far, bf16[2,112,384]{2,1,0:T(8,128)(2,1)S(1)} %get-tuple-element.17.middle, ...), custom_call_target="tpu_custom_call" | custom-call | flops 891813888 | bytes 4194304 | tf_op jit(solution)/shard_map/pallas_call | solution.py:188
  137.8 0.6 collective-permute-start.33
  138.3 4.2 %collective-permute-start.34 = (bf16[2,112,384]{2,1,0:T(8,128)(2,1)S(1)}, bf16[2,112,384]{2,1,0:T(8,128)(2,1)S(1)}, u32[]{:S(2)}, u32[]{:S(2)}) collective-permute-start(bf16[2,112,384]{2,1,0:T(8,128)(2,1)S(1)} %shard_map.117.grad), channel_id=1, source_target_pairs={{1,2},{3,4},{5,6},{7,8},{9,10},{11,12},{13,14},{2,1},{4,3},{6,5},{... | collective-permute-start | bytes 516104 | tf_op jit(solution)/shard_map/ppermute | solution.py:294
  142.6 4.6 %shard_map.118 = (bf16[2,112,384]{2,1,0:T(8,128)(2,1)}, f32[3,224,384]{2,1,0:T(8,128)S(1)}) custom-call(bf16[2,112,384]{2,1,0:T(8,128)(2,1)S(1)} %bitcast.32, bf16[2,112,384]{2,1,0:T(8,128)(2,1)S(1)} %get-tuple-element.16.act, bf16[8,112,384]{2,1,0:T(8,128)(2,1)S(1)} %collective-permute-done.near, bf16[8,112,384]{2,1,0:T(8,128)(2,1)S(1)} %collective-permute-done.1.far, ...), custom_call_target="tpu_custom_call" | custom-call | flops 1981808640 | bytes 4194304 | tf_op jit(solution)/shard_map/pallas_call | solution.py:188
  147.3 2.1 %shard_map.119 = bf16[2,112,384]{2,1,0:T(8,128)(2,1)} custom-call(bf16[2,112,384]{2,1,0:T(8,128)(2,1)S(1)} %collective-permute-done.33.near, bf16[2,112,384]{2,1,0:T(8,128)(2,1)S(1)} %collective-permute-done.34.far, bf16[2,112,384]{2,1,0:T(8,128)(2,1)S(1)} %bitcast.19, bf16[2,112,384]{2,1,0:T(8,128)(2,1)S(1)} %bitcast.22, f32[384]{0:T(512)S(1)} %copy-done.7, ...), custom_call_target="tpu_custom_call" | custom-call | flops 594542592 | bytes 4194304 | tf_op jit(solution)/shard_map/pallas_call | solution.py:188
  (63 shorter events, 1.0 us)
Async XLA Ops:
  0.6 117.0 %copy-start.3 = (bf16[10368,24]{0,1:T(8,128)(2,1)S(1)}, bf16[10368,24]{0,1:T(8,128)(2,1)}, u32[]{:S(2)}) copy-start(bf16[10368,24]{0,1:T(8,128)(2,1)} %param.17) | copy-start | bytes 1492996
  0.6 117.0 %copy-start.2 = (bf16[10368,24]{0,1:T(8,128)(2,1)S(1)}, bf16[10368,24]{0,1:T(8,128)(2,1)}, u32[]{:S(2)}) copy-start(bf16[10368,24]{0,1:T(8,128)(2,1)} %param.18) | copy-start | bytes 1492996
  0.7 116.6 %copy-start = (bf16[2,1,112,384]{3,2,1,0:T(8,128)(2,1)S(1)}, bf16[2,1,112,384]{3,2,1,0:T(8,128)(2,1)}, u32[]{:S(2)}) copy-start(bf16[2,1,112,384]{3,2,1,0:T(8,128)(2,1)} %param.10) | copy-start | bytes 516100
  0.7 116.6 %copy-start.4 = (bf16[2,1,112,384]{3,2,1,0:T(8,128)(2,1)S(1)}, bf16[2,1,112,384]{3,2,1,0:T(8,128)(2,1)}, u32[]{:S(2)}) copy-start(bf16[2,1,112,384]{3,2,1,0:T(8,128)(2,1)} %param.11) | copy-start | bytes 516100
  0.7 116.6 %copy-start.7 = (f32[384]{0:T(512)S(1)}, f32[384]{0:T(512)}, u32[]{:S(2)}) copy-start(f32[384]{0:T(512)} %gain.7) | copy-start | bytes 4612
  2.6 7.6 %collective-permute-start.11 = (bf16[48,2176]{1,0:T(8,128)(2,1)S(1)}, bf16[48,2176]{1,0:T(8,128)(2,1)S(1)}, u32[]{:S(2)}, u32[]{:S(2)}) collective-permute-start(bf16[48,2176]{1,0:T(8,128)(2,1)S(1)} %pad_maximum_fusion.3), channel_id=1, source_target_pairs={{0,2},{1,3},{2,0},{3,1},{4,6},{5,7},{6,4},{7,5},{8,10},{9,11},{10,... | collective-permute-start | bytes 626696 | tf_op jit(solution)/shard_map/ppermute | solution.py:240
  4.6 12.1 %collective-permute-start.2 = (bf16[48,4096]{1,0:T(8,128)(2,1)S(1)}, bf16[48,4096]{1,0:T(8,128)(2,1)S(1)}, u32[]{:S(2)}, u32[]{:S(2)}) collective-permute-start(bf16[48,4096]{1,0:T(8,128)(2,1)S(1)} %pad_maximum_fusion.2), channel_id=1, source_target_pairs={{0,4},{1,5},{2,6},{3,7},{4,8},{5,9},{6,10},{7,11},{8,12},{9,13},{1... | collective-permute-start | bytes 1179656 | tf_op jit(solution)/shard_map/ppermute | solution.py:239
  6.2 12.1 %collective-permute-start.20 = (bf16[48,4096]{1,0:T(8,128)(2,1)S(1)}, bf16[48,4096]{1,0:T(8,128)(2,1)S(1)}, u32[]{:S(2)}, u32[]{:S(2)}) collective-permute-start(bf16[48,4096]{1,0:T(8,128)(2,1)S(1)} %pad_maximum_fusion.2), channel_id=1, source_target_pairs={{0,2},{1,3},{2,0},{3,1},{4,6},{5,7},{6,4},{7,5},{8,10},{9,11},{10,... | collective-permute-start | bytes 1179656 | tf_op jit(solution)/shard_map/ppermute | solution.py:240
  7.4 24.7 %collective-permute-start.17 = (bf16[24,10368]{1,0:T(8,128)(2,1)}, bf16[24,10368]{1,0:T(8,128)(2,1)S(1)}, u32[]{:S(2)}, u32[]{:S(2)}) collective-permute-start(bf16[24,10368]{1,0:T(8,128)(2,1)} %bitcast.27), channel_id=1, source_target_pairs={{0,1},{1,0},{2,3},{3,2},{4,5},{5,4},{6,7},{7,6},{8,9},{9,8},{10,11... | collective-permute-start | bytes 1493000 | tf_op jit(solution)/shard_map/ppermute | solution.py:241
  8.9 23.3 %collective-permute-start.18 = (bf16[24,10368]{1,0:T(8,128)(2,1)}, bf16[24,10368]{1,0:T(8,128)(2,1)S(1)}, u32[]{:S(2)}, u32[]{:S(2)}) collective-permute-start(bf16[24,10368]{1,0:T(8,128)(2,1)} %bitcast.24), channel_id=1, source_target_pairs={{0,1},{1,0},{2,3},{3,2},{4,5},{5,4},{6,7},{7,6},{8,9},{9,8},{10,11... | collective-permute-start | bytes 1493000 | tf_op jit(solution)/shard_map/ppermute | solution.py:241
  10.2 39.1 %collective-permute-start = (bf16[8,112,384]{2,1,0:T(8,128)(2,1)S(1)}, bf16[8,112,384]{2,1,0:T(8,128)(2,1)S(1)}, u32[]{:S(2)}, u32[]{:S(2)}) collective-permute-start(bf16[8,112,384]{2,1,0:T(8,128)(2,1)S(1)} %pad_maximum_fusion), channel_id=1, source_target_pairs={{0,1},{1,0},{2,3},{3,2},{4,5},{5,4},{6,7},{7,6},{8,9},{9,8},{10,11... | collective-permute-start | bytes 2064392 | tf_op jit(solution)/shard_map/ppermute | solution.py:293
  16.7 2.6 %collective-permute-start.19 = (bf16[48,2176]{1,0:T(8,128)(2,1)S(1)}, bf16[48,2176]{1,0:T(8,128)(2,1)S(1)}, u32[]{:S(2)}, u32[]{:S(2)}) collective-permute-start(bf16[48,2176]{1,0:T(8,128)(2,1)S(1)} %collective-permute-done.11.refs_4_), channel_id=1, source_target_pairs={{0,1},{1,0},{2,3},{3,2},{4,5},{5,4},{6,7},{7,6},{8,9},{9,8},{10,11... | collective-permute-start | bytes 626696 | tf_op jit(solution)/shard_map/ppermute | solution.py:241
  18.3 12.2 %collective-permute-start.3 = (bf16[48,4096]{1,0:T(8,128)(2,1)S(1)}, bf16[48,4096]{1,0:T(8,128)(2,1)S(1)}, u32[]{:S(2)}, u32[]{:S(2)}) collective-permute-start(bf16[48,4096]{1,0:T(8,128)(2,1)S(1)} %collective-permute-done.2), channel_id=1, source_target_pairs={{0,4},{1,5},{2,6},{3,7},{4,8},{5,9},{6,10},{7,11},{8,12},{9,13},{1... | collective-permute-start | bytes 1179656 | tf_op jit(solution)/shard_map/ppermute | solution.py:239
  19.4 31.4 %collective-permute-start.1 = (bf16[8,112,384]{2,1,0:T(8,128)(2,1)S(1)}, bf16[8,112,384]{2,1,0:T(8,128)(2,1)S(1)}, u32[]{:S(2)}, u32[]{:S(2)}) collective-permute-start(bf16[8,112,384]{2,1,0:T(8,128)(2,1)S(1)} %pad_maximum_fusion), channel_id=1, source_target_pairs={{1,2},{3,4},{5,6},{7,8},{9,10},{11,12},{13,14},{2,1},{4,3},{6,5},{... | collective-permute-start | bytes 2064392 | tf_op jit(solution)/shard_map/ppermute | solution.py:294
  30.5 17.4 %collective-permute-start.25 = (bf16[48,4096]{1,0:T(8,128)(2,1)S(1)}, bf16[48,4096]{1,0:T(8,128)(2,1)S(1)}, u32[]{:S(2)}, u32[]{:S(2)}) collective-permute-start(bf16[48,4096]{1,0:T(8,128)(2,1)S(1)} %collective-permute-done.2), channel_id=1, source_target_pairs={{0,2},{1,3},{2,0},{3,1},{4,6},{5,7},{6,4},{7,5},{8,10},{9,11},{10,... | collective-permute-start | bytes 1179656 | tf_op jit(solution)/shard_map/ppermute | solution.py:240
  32.2 17.1 %collective-permute-start.12 = (bf16[96,2176]{1,0:T(8,128)(2,1)S(1)}, bf16[96,2176]{1,0:T(8,128)(2,1)S(1)}, u32[]{:S(2)}, u32[]{:S(2)}) collective-permute-start(bf16[96,2176]{1,0:T(8,128)(2,1)S(1)} %pad_maximum_fusion.1), channel_id=1, source_target_pairs={{0,4},{1,5},{2,6},{3,7},{4,8},{5,9},{6,10},{7,11},{8,12},{9,13},{1... | collective-permute-start | bytes 1253384 | tf_op jit(solution)/shard_map/ppermute | solution.py:239
  32.2 39.6 %collective-permute-start.22 = (bf16[96,4096]{1,0:T(8,128)(2,1)S(1)}, bf16[96,4096]{1,0:T(8,128)(2,1)S(1)}, u32[]{:S(2)}, u32[]{:S(2)}) collective-permute-start(bf16[96,4096]{1,0:T(8,128)(2,1)S(1)} %constant_dynamic-update-slice_fusion.2.refs_6_), channel_id=1, source_target_pairs={{0,16},{16,0},{1,17},{17,1},{2,18},{18,2},{3,19},{19,3},{4,20},{20... | collective-permute-start | bytes 2359304 | tf_op jit(solution)/shard_map/ppermute | solution.py:242
  48.0 12.0 %collective-permute-start.4 = (bf16[48,4096]{1,0:T(8,128)(2,1)S(1)}, bf16[48,4096]{1,0:T(8,128)(2,1)S(1)}, u32[]{:S(2)}, u32[]{:S(2)}) collective-permute-start(bf16[48,4096]{1,0:T(8,128)(2,1)S(1)} %collective-permute-done.3), channel_id=1, source_target_pairs={{0,4},{1,5},{2,6},{3,7},{4,8},{5,9},{6,10},{7,11},{8,12},{9,13},{1... | collective-permute-start | bytes 1179656 | tf_op jit(solution)/shard_map/ppermute | solution.py:239
  49.3 22.6 %collective-permute-start.21 = (bf16[96,4096]{1,0:T(8,128)(2,1)S(1)}, bf16[96,4096]{1,0:T(8,128)(2,1)S(1)}, u32[]{:S(2)}, u32[]{:S(2)}) collective-permute-start(bf16[96,4096]{1,0:T(8,128)(2,1)S(1)} %constant_dynamic-update-slice_fusion.2.refs_6_), channel_id=1, source_target_pairs={{0,1},{1,0},{2,3},{3,2},{4,5},{5,4},{6,7},{7,6},{8,9},{9,8},{10,11... | collective-permute-start | bytes 2359304 | tf_op jit(solution)/shard_map/ppermute | solution.py:241
  49.4 19.5 %collective-permute-start.13 = (bf16[96,2176]{1,0:T(8,128)(2,1)S(1)}, bf16[96,2176]{1,0:T(8,128)(2,1)S(1)}, u32[]{:S(2)}, u32[]{:S(2)}) collective-permute-start(bf16[96,2176]{1,0:T(8,128)(2,1)S(1)} %collective-permute-done.12.refs_10_), channel_id=1, source_target_pairs={{0,4},{1,5},{2,6},{3,7},{4,8},{5,9},{6,10},{7,11},{8,12},{9,13},{1... | collective-permute-start | bytes 1253384 | tf_op jit(solution)/shard_map/ppermute | solution.py:239
  50.7 19.4 %collective-permute-start.24 = (bf16[96,2176]{1,0:T(8,128)(2,1)S(1)}, bf16[96,2176]{1,0:T(8,128)(2,1)S(1)}, u32[]{:S(2)}, u32[]{:S(2)}) collective-permute-start(bf16[96,2176]{1,0:T(8,128)(2,1)S(1)} %collective-permute-done.12.refs_10_), channel_id=1, source_target_pairs={{0,1},{1,0},{2,3},{3,2},{4,5},{5,4},{6,7},{7,6},{8,9},{9,8},{10,11... | collective-permute-start | bytes 1253384 | tf_op jit(solution)/shard_map/ppermute | solution.py:241
  59.9 11.8 %collective-permute-start.8 = (bf16[48,4096]{1,0:T(8,128)(2,1)S(1)}, bf16[48,4096]{1,0:T(8,128)(2,1)S(1)}, u32[]{:S(2)}, u32[]{:S(2)}) collective-permute-start(bf16[48,4096]{1,0:T(8,128)(2,1)S(1)} %collective-permute-done.3), channel_id=1, source_target_pairs={{0,2},{1,3},{2,0},{3,1},{4,6},{5,7},{6,4},{7,5},{8,10},{9,11},{10,... | collective-permute-start | bytes 1179656 | tf_op jit(solution)/shard_map/ppermute | solution.py:240
  68.9 17.8 %collective-permute-start.27 = (bf16[96,4096]{1,0:T(8,128)(2,1)S(1)}, bf16[96,4096]{1,0:T(8,128)(2,1)S(1)}, u32[]{:S(2)}, u32[]{:S(2)}) collective-permute-start(bf16[96,4096]{1,0:T(8,128)(2,1)S(1)} %constant_dynamic-update-slice_fusion.4.refs_12_), channel_id=1, source_target_pairs={{0,16},{16,0},{1,17},{17,1},{2,18},{18,2},{3,19},{19,3},{4,20},{20... | collective-permute-start | bytes 2359304 | tf_op jit(solution)/shard_map/ppermute | solution.py:242
  70.1 16.5 %collective-permute-start.26 = (bf16[96,4096]{1,0:T(8,128)(2,1)S(1)}, bf16[96,4096]{1,0:T(8,128)(2,1)S(1)}, u32[]{:S(2)}, u32[]{:S(2)}) collective-permute-start(bf16[96,4096]{1,0:T(8,128)(2,1)S(1)} %constant_dynamic-update-slice_fusion.4.refs_12_), channel_id=1, source_target_pairs={{0,1},{1,0},{2,3},{3,2},{4,5},{5,4},{6,7},{7,6},{8,9},{9,8},{10,11... | collective-permute-start | bytes 2359304 | tf_op jit(solution)/shard_map/ppermute | solution.py:241
  71.7 2.5 %collective-permute-start.29 = (bf16[96,2176]{1,0:T(8,128)(2,1)S(1)}, bf16[96,2176]{1,0:T(8,128)(2,1)S(1)}, u32[]{:S(2)}, u32[]{:S(2)}) collective-permute-start(bf16[96,2176]{1,0:T(8,128)(2,1)S(1)} %collective-permute-done.13.refs_16_), channel_id=1, source_target_pairs={{0,1},{1,0},{2,3},{3,2},{4,5},{5,4},{6,7},{7,6},{8,9},{9,8},{10,11... | collective-permute-start | bytes 1253384 | tf_op jit(solution)/shard_map/ppermute | solution.py:241
  71.8 12.6 %collective-permute-start.14 = (bf16[96,2176]{1,0:T(8,128)(2,1)S(1)}, bf16[96,2176]{1,0:T(8,128)(2,1)S(1)}, u32[]{:S(2)}, u32[]{:S(2)}) collective-permute-start(bf16[96,2176]{1,0:T(8,128)(2,1)S(1)} %collective-permute-done.13.refs_16_), channel_id=1, source_target_pairs={{0,4},{1,5},{2,6},{3,7},{4,8},{5,9},{6,10},{7,11},{8,12},{9,13},{1... | collective-permute-start | bytes 1253384 | tf_op jit(solution)/shard_map/ppermute | solution.py:239
  71.9 31.6 %collective-permute-start.9 = (bf16[96,4096]{1,0:T(8,128)(2,1)S(1)}, bf16[96,4096]{1,0:T(8,128)(2,1)S(1)}, u32[]{:S(2)}, u32[]{:S(2)}) collective-permute-start(bf16[96,4096]{1,0:T(8,128)(2,1)S(1)} %constant_dynamic-update-slice_fusion.refs_18_), channel_id=1, source_target_pairs={{0,16},{16,0},{1,17},{17,1},{2,18},{18,2},{3,19},{19,3},{4,20},{20... | collective-permute-start | bytes 2359304 | tf_op jit(solution)/shard_map/ppermute | solution.py:242
  74.2 32.7 %collective-permute-start.30 = (bf16[96,4096]{1,0:T(8,128)(2,1)S(1)}, bf16[96,4096]{1,0:T(8,128)(2,1)S(1)}, u32[]{:S(2)}, u32[]{:S(2)}) collective-permute-start(bf16[96,4096]{1,0:T(8,128)(2,1)S(1)} %constant_dynamic-update-slice_fusion.refs_18_), channel_id=1, source_target_pairs={{0,1},{1,0},{2,3},{3,2},{4,5},{5,4},{6,7},{7,6},{8,9},{9,8},{10,11... | collective-permute-start | bytes 2359304 | tf_op jit(solution)/shard_map/ppermute | solution.py:241
  84.4 22.8 %collective-permute-start.23 = (bf16[96,4096]{1,0:T(8,128)(2,1)S(1)}, bf16[96,4096]{1,0:T(8,128)(2,1)S(1)}, u32[]{:S(2)}, u32[]{:S(2)}) collective-permute-start(bf16[96,4096]{1,0:T(8,128)(2,1)S(1)} %collective-permute-done.22.refs_8_), channel_id=1, source_target_pairs={{0,1},{1,0},{2,3},{3,2},{4,5},{5,4},{6,7},{7,6},{8,9},{9,8},{10,11... | collective-permute-start | bytes 2359304 | tf_op jit(solution)/shard_map/ppermute | solution.py:241
  86.6 19.1 %collective-permute-start.5 = (bf16[48,4096]{1,0:T(8,128)(2,1)S(1)}, bf16[48,4096]{1,0:T(8,128)(2,1)S(1)}, u32[]{:S(2)}, u32[]{:S(2)}) collective-permute-start(bf16[48,4096]{1,0:T(8,128)(2,1)S(1)} %collective-permute-done.4), channel_id=1, source_target_pairs={{0,2},{1,3},{2,0},{3,1},{4,6},{5,7},{6,4},{7,5},{8,10},{9,11},{10,... | collective-permute-start | bytes 1179656 | tf_op jit(solution)/shard_map/ppermute | solution.py:240
  86.7 31.0 %collective-permute-start.28 = (bf16[96,4096]{1,0:T(8,128)(2,1)S(1)}, bf16[96,4096]{1,0:T(8,128)(2,1)S(1)}, u32[]{:S(2)}, u32[]{:S(2)}) collective-permute-start(bf16[96,4096]{1,0:T(8,128)(2,1)S(1)} %collective-permute-done.27.refs_14_), channel_id=1, source_target_pairs={{0,1},{1,0},{2,3},{3,2},{4,5},{5,4},{6,7},{7,6},{8,9},{9,8},{10,11... | collective-permute-start | bytes 2359304 | tf_op jit(solution)/shard_map/ppermute | solution.py:241
  103.5 22.6 %collective-permute-start.10 = (bf16[96,4096]{1,0:T(8,128)(2,1)S(1)}, bf16[96,4096]{1,0:T(8,128)(2,1)S(1)}, u32[]{:S(2)}, u32[]{:S(2)}) collective-permute-start(bf16[96,4096]{1,0:T(8,128)(2,1)S(1)} %collective-permute-done.9.refs_0_), channel_id=1, source_target_pairs={{0,1},{1,0},{2,3},{3,2},{4,5},{5,4},{6,7},{7,6},{8,9},{9,8},{10,11... | collective-permute-start | bytes 2359304 | tf_op jit(solution)/shard_map/ppermute | solution.py:241
  105.7 10.7 %collective-permute-start.6 = (bf16[48,4096]{1,0:T(8,128)(2,1)S(1)}, bf16[48,4096]{1,0:T(8,128)(2,1)S(1)}, u32[]{:S(2)}, u32[]{:S(2)}) collective-permute-start(bf16[48,4096]{1,0:T(8,128)(2,1)S(1)} %collective-permute-done.5.refs_4_), channel_id=1, source_target_pairs={{0,16},{16,0},{1,17},{17,1},{2,18},{18,2},{3,19},{19,3},{4,20},{20... | collective-permute-start | bytes 1179656 | tf_op jit(solution)/shard_map/ppermute | solution.py:242
  106.9 19.2 %collective-permute-start.15 = (bf16[96,2176]{1,0:T(8,128)(2,1)S(1)}, bf16[96,2176]{1,0:T(8,128)(2,1)S(1)}, u32[]{:S(2)}, u32[]{:S(2)}) collective-permute-start(bf16[96,2176]{1,0:T(8,128)(2,1)S(1)} %collective-permute-done.14.refs_2_), channel_id=1, source_target_pairs={{0,1},{1,0},{2,3},{3,2},{4,5},{5,4},{6,7},{7,6},{8,9},{9,8},{10,11... | collective-permute-start | bytes 1253384 | tf_op jit(solution)/shard_map/ppermute | solution.py:241
  107.2 18.9 %collective-permute-start.16 = (bf16[48,4096]{1,0:T(8,128)(2,1)S(1)}, bf16[48,4096]{1,0:T(8,128)(2,1)S(1)}, u32[]{:S(2)}, u32[]{:S(2)}) collective-permute-start(bf16[48,4096]{1,0:T(8,128)(2,1)S(1)} %collective-permute-done.5.refs_4_), channel_id=1, source_target_pairs={{0,1},{1,0},{2,3},{3,2},{4,5},{5,4},{6,7},{7,6},{8,9},{9,8},{10,11... | collective-permute-start | bytes 1179656 | tf_op jit(solution)/shard_map/ppermute | solution.py:241
  116.4 11.7 %collective-permute-start.7 = (bf16[48,4096]{1,0:T(8,128)(2,1)S(1)}, bf16[48,4096]{1,0:T(8,128)(2,1)S(1)}, u32[]{:S(2)}, u32[]{:S(2)}) collective-permute-start(bf16[48,4096]{1,0:T(8,128)(2,1)S(1)} %collective-permute-done.6.refs_0_), channel_id=1, source_target_pairs={{0,1},{1,0},{2,3},{3,2},{4,5},{5,4},{6,7},{7,6},{8,9},{9,8},{10,11... | collective-permute-start | bytes 1179656 | tf_op jit(solution)/shard_map/ppermute | solution.py:241
  126.1 1.9 %copy-start.6 = (f32[384]{0:T(512)S(1)}, f32[384]{0:T(512)}, u32[]{:S(2)}) copy-start(f32[384]{0:T(512)} %gain.6) | copy-start | bytes 4612
  126.1 1.9 %copy-start.8 = (f32[384]{0:T(512)S(1)}, f32[384]{0:T(512)}, u32[]{:S(2)}) copy-start(f32[384]{0:T(512)} %bias.2) | copy-start | bytes 4612
  128.1 7.9 %copy-start.1 = (bf16[2,1,112,384]{3,2,1,0:T(8,128)(2,1)S(1)}, bf16[2,1,112,384]{3,2,1,0:T(8,128)(2,1)}, u32[]{:S(2)}) copy-start(bf16[2,1,112,384]{3,2,1,0:T(8,128)(2,1)} %param.19) | copy-start | bytes 516100
  133.9 8.7 %copy-start.5 = (bf16[2,1,112,384]{3,2,1,0:T(8,128)(2,1)S(1)}, bf16[2,1,112,384]{3,2,1,0:T(8,128)(2,1)}, u32[]{:S(2)}) copy-start(bf16[2,1,112,384]{3,2,1,0:T(8,128)(2,1)} %param.12) | copy-start | bytes 516100
  133.9 8.7 %copy-start.9 = (f32[384]{0:T(512)S(1)}, f32[384]{0:T(512)}, u32[]{:S(2)}) copy-start(f32[384]{0:T(512)} %bias.3) | copy-start | bytes 4612
  133.9 8.7 %collective-permute-start.31 = (bf16[2,112,384]{2,1,0:T(8,128)(2,1)S(1)}, bf16[2,112,384]{2,1,0:T(8,128)(2,1)S(1)}, u32[]{:S(2)}, u32[]{:S(2)}) collective-permute-start(bf16[2,112,384]{2,1,0:T(8,128)(2,1)S(1)} %get-tuple-element.16.act), channel_id=1, source_target_pairs={{0,1},{1,0},{2,3},{3,2},{4,5},{5,4},{6,7},{7,6},{8,9},{9,8},{10,11... | collective-permute-start | bytes 516104 | tf_op jit(solution)/shard_map/ppermute | solution.py:293
  134.0 8.6 %collective-permute-start.32 = (bf16[2,112,384]{2,1,0:T(8,128)(2,1)S(1)}, bf16[2,112,384]{2,1,0:T(8,128)(2,1)S(1)}, u32[]{:S(2)}, u32[]{:S(2)}) collective-permute-start(bf16[2,112,384]{2,1,0:T(8,128)(2,1)S(1)} %get-tuple-element.16.act), channel_id=1, source_target_pairs={{1,2},{3,4},{5,6},{7,8},{9,10},{11,12},{13,14},{2,1},{4,3},{6,5},{... | collective-permute-start | bytes 516104 | tf_op jit(solution)/shard_map/ppermute | solution.py:294
  137.8 9.5 %collective-permute-start.33 = (bf16[2,112,384]{2,1,0:T(8,128)(2,1)S(1)}, bf16[2,112,384]{2,1,0:T(8,128)(2,1)S(1)}, u32[]{:S(2)}, u32[]{:S(2)}) collective-permute-start(bf16[2,112,384]{2,1,0:T(8,128)(2,1)S(1)} %shard_map.117.grad), channel_id=1, source_target_pairs={{0,1},{1,0},{2,3},{3,2},{4,5},{5,4},{6,7},{7,6},{8,9},{9,8},{10,11... | collective-permute-start | bytes 516104 | tf_op jit(solution)/shard_map/ppermute | solution.py:293
  138.3 8.9 %collective-permute-start.34 = (bf16[2,112,384]{2,1,0:T(8,128)(2,1)S(1)}, bf16[2,112,384]{2,1,0:T(8,128)(2,1)S(1)}, u32[]{:S(2)}, u32[]{:S(2)}) collective-permute-start(bf16[2,112,384]{2,1,0:T(8,128)(2,1)S(1)} %shard_map.117.grad), channel_id=1, source_target_pairs={{1,2},{3,4},{5,6},{7,8},{9,10},{11,12},{13,14},{2,1},{4,3},{6,5},{... | collective-permute-start | bytes 516104 | tf_op jit(solution)/shard_map/ppermute | solution.py:294
